TPU v7x, 16 devices: a whole 2x2x2 slice. The times are simulated.
16 devices in a mesh: dpz: 2 (over z), dpy: 2 (over y), dpx: 4 (over x, core).
Axes of the slice: x: 2, y: 2, z: 2, core: 2. Of those that a mesh axis runs over, the one named last changes fastest.
Arguments:
- x_in: bfloat16 [65536, 768], P(('dpz', 'dpy', 'dpx'))
- dy_out: bfloat16 [65536, 768], P(('dpz', 'dpy', 'dpx'))
- w1_in: bfloat16 [768, 3072], replicated
- w1_out: bfloat16 [3072, 768], replicated
- w2_in: bfloat16 [768, 3072], replicated
- w2_out: bfloat16 [3072, 768], replicated
- master: float32 [9437184], P(('dpz', 'dpy', 'dpx'))
- adam_m: float32 [9437184], P(('dpz', 'dpy', 'dpx'))
- adam_v: float32 [9437184], P(('dpz', 'dpy', 'dpx'))
Outputs:
- output 1: float32 [9437184], P(('dpz', 'dpy', 'dpx'))
- output 2: float32 [9437184], P(('dpz', 'dpy', 'dpx'))
- output 3: float32 [9437184], P(('dpz', 'dpy', 'dpx'))
- output 4: bfloat16 [9437184], replicated
All inputs are finite; a program needn't handle non-finite values.
Results may differ from a plain program's by a relative error of at most 0.00931221.
Values are sent between devices in bfloat16 or wider.
A program may use at most 1 GiB of HBM per device.

v0:
```python
import math
import jax
import jax.numpy as jnp
from jax import lax
from jax.sharding import PartitionSpec as P, NamedSharding

AXES = ('dpz', 'dpy', 'dpx')
STEP = 10
BETA_ONE = 0.9
BETA_TWO = 0.999
LEARN_RATE = 0.001
ADAM_EPS = 1e-8


def gelu_value(z_val):
    return 0.5 * z_val * (1.0 + lax.erf(z_val * (1.0 / math.sqrt(2.0))))


def gelu_slope(z_val):
    cdf_part = 0.5 * (1.0 + lax.erf(z_val * (1.0 / math.sqrt(2.0))))
    return cdf_part + z_val * jnp.exp(-0.5 * z_val * z_val) * (1.0 / math.sqrt(2.0 * math.pi))


def device_grads(x_one, dy_one, w1_in, w1_out, w2_in, w2_out):
    z_one = jnp.dot(x_one, w1_in, preferred_element_type=jnp.float32).astype(jnp.bfloat16)
    h_one = gelu_value(z_one.astype(jnp.float32)).astype(jnp.bfloat16)
    x_two = (x_one.astype(jnp.float32) + jnp.dot(h_one, w1_out, preferred_element_type=jnp.float32)).astype(jnp.bfloat16)
    z_two = jnp.dot(x_two, w2_in, preferred_element_type=jnp.float32).astype(jnp.bfloat16)
    h_two = gelu_value(z_two.astype(jnp.float32)).astype(jnp.bfloat16)
    g2_out = jnp.einsum('tf,td->fd', h_two, dy_one, preferred_element_type=jnp.float32).astype(jnp.bfloat16)
    dz_two = (jnp.einsum('td,fd->tf', dy_one, w2_out, preferred_element_type=jnp.float32) * gelu_slope(z_two.astype(jnp.float32))).astype(jnp.bfloat16)
    g2_in = jnp.einsum('td,tf->df', x_two, dz_two, preferred_element_type=jnp.float32).astype(jnp.bfloat16)
    dx_two = (dy_one.astype(jnp.float32) + jnp.einsum('tf,df->td', dz_two, w2_in, preferred_element_type=jnp.float32)).astype(jnp.bfloat16)
    g1_out = jnp.einsum('tf,td->fd', h_one, dx_two, preferred_element_type=jnp.float32).astype(jnp.bfloat16)
    dz_one = (jnp.einsum('td,fd->tf', dx_two, w1_out, preferred_element_type=jnp.float32) * gelu_slope(z_one.astype(jnp.float32))).astype(jnp.bfloat16)
    g1_in = jnp.einsum('td,tf->df', x_one, dz_one, preferred_element_type=jnp.float32).astype(jnp.bfloat16)
    return jnp.concatenate([g2_out.reshape(-1), g2_in.reshape(-1), g1_out.reshape(-1), g1_in.reshape(-1)])


def solution(mesh):
    size_z = mesh.shape['dpz']
    size_y = mesh.shape['dpy']
    size_x = mesh.shape['dpx']

    def local_step(x_one, dy_one, w1_in, w1_out, w2_in, w2_out, master, adam_m, adam_v):
        flat_grads = device_grads(x_one, dy_one, w1_in, w1_out, w2_in, w2_out)
        shard_len = flat_grads.shape[0] // (size_z * size_y * size_x)
        grad_grid = flat_grads.reshape(size_z * size_y, size_x, shard_len)
        received = lax.all_to_all(grad_grid, 'dpx', 1, 1, tiled=True)
        part_x = jnp.sum(received, axis=1, dtype=jnp.float32)
        part_y = lax.psum_scatter(part_x.reshape(size_z, size_y, shard_len), 'dpy', scatter_dimension=1, tiled=True)
        part_z = lax.psum_scatter(part_y, 'dpz', scatter_dimension=0, tiled=True)
        grad_shard = part_z.reshape(shard_len)
        new_m = BETA_ONE * adam_m + (1.0 - BETA_ONE) * grad_shard
        new_v = BETA_TWO * adam_v + (1.0 - BETA_TWO) * grad_shard * grad_shard
        m_hat = new_m / (1.0 - BETA_ONE ** STEP)
        v_hat = new_v / (1.0 - BETA_TWO ** STEP)
        new_master = master - LEARN_RATE * m_hat / (jnp.sqrt(v_hat) + ADAM_EPS)
        weights_bf = lax.all_gather(new_master.astype(jnp.bfloat16), AXES, tiled=True)
        return new_master, new_m, new_v, weights_bf

    in_specs = (P(AXES, None), P(AXES, None), P(), P(), P(), P(), P(AXES), P(AXES), P(AXES))
    out_specs = (P(AXES), P(AXES), P(AXES), P())
    return jax.shard_map(local_step, mesh=mesh, in_specs=in_specs, out_specs=out_specs, check_vma=False)
```

profile of v0, /device:TPU:0, one launch (start us, length us, event | category | flops | bytes accessed | tf_op | source)
XLA Modules:
  0.0 1146.4 jit_solution(12961781500097499526)
XLA Ops:
  7.2 33.4 %fusion.3 = (f32[4096,3072]{1,0:T(8,128)}, bf16[4096,3072]{1,0:T(8,128)(2,1)}) fusion(bf16[4096,768]{1,0:T(8,128)(2,1)} %param.9, bf16[768,3072]{1,0:T(8,128)(2,1)} %param.11), kind=kOutput, calls=%fused_computation.13 | convolution fusion | flops 19377684480 | bytes 86507520 | tf_op jit(solution)/shard_map/dot_general | solution.py:25
  40.6 35.3 %add_convert_fusion.1 = bf16[4096,768]{1,0:T(8,128)(2,1)} fusion(bf16[4096,768]{1,0:T(8,128)(2,1)} %param.9, bf16[3072,768]{1,0:T(8,128)(2,1)} %param.12, f32[4096,3072]{1,0:T(8,128)} %get-tuple-element.8, bf16[4096,3072]{1,0:T(8,128)(2,1)} %get-tuple-element.9), kind=kOutput, calls=%fused_computation.36 | convolution fusion | flops 19387121664 | bytes 92798976 | tf_op jit(solution)/shard_map/dot_general | solution.py:27
  75.9 27.1 %convolution_convert_fusion = bf16[4096,3072]{1,0:T(8,128)(2,1)} fusion(bf16[4096,768]{1,0:T(8,128)(2,1)} %add_convert_fusion.1, bf16[768,3072]{1,0:T(8,128)(2,1)} %param.13), kind=kOutput, calls=%fused_computation.31 | convolution fusion | flops 19339935744 | bytes 36175872 | tf_op jit(solution)/shard_map/dot_general | solution.py:28
  103.0 25.4 %fusion.23 = bf16[3072,768]{1,0:T(8,128)(2,1)} fusion(bf16[4096,768]{1,0:T(8,128)(2,1)S(1)} %copy-done.1, bf16[4096,3072]{1,0:T(8,128)(2,1)} %convolution_convert_fusion), kind=kOutput, calls=%fused_computation.38 | convolution fusion | flops 19405209600 | bytes 36175872 | tf_op jit(solution)/shard_map/tf,td->fd/dot_general | solution.py:30
  128.4 37.6 %fusion.17 = bf16[4096,3072]{1,0:T(8,128)(2,1)} fusion(bf16[4096,3072]{1,0:T(8,128)(2,1)} %convolution_convert_fusion, bf16[4096,768]{1,0:T(8,128)(2,1)S(1)} %copy-done.1, bf16[3072,768]{1,0:T(8,128)(2,1)S(1)} %bitcast.29), kind=kOutput, calls=%fused_computation.27 | convolution fusion | flops 19465764864 | bytes 61341696 | tf_op jit(solution)/shard_map/td,fd->tf/dot_general | solution.py:31
  166.0 25.0 %convolution_convert_fusion.3 = bf16[768,3072]{1,0:T(8,128)(2,1)} fusion(bf16[4096,768]{1,0:T(8,128)(2,1)S(1)} %bitcast.31, bf16[4096,3072]{1,0:T(8,128)(2,1)} %fusion.17), kind=kOutput, calls=%fused_computation.40 | convolution fusion | flops 19329712128 | bytes 36175872 | tf_op jit(solution)/shard_map/td,tf->df/dot_general | solution.py:32
  191.0 25.6 %add_convert_fusion = bf16[4096,768]{1,0:T(8,128)(2,1)} fusion(bf16[4096,768]{1,0:T(8,128)(2,1)S(1)} %copy-done.1, bf16[4096,3072]{1,0:T(8,128)(2,1)} %fusion.17, bf16[768,3072]{1,0:T(8,128)(2,1)} %param.13), kind=kOutput, calls=%fused_computation.35 | convolution fusion | flops 19336790016 | bytes 42467328 | tf_op jit(solution)/shard_map/tf,df->td/dot_general | solution.py:33
  216.6 65.4 %fusion.26 = bf16[768,3072]{0,1:T(8,128)(2,1)} fusion(bf16[4096,768]{1,0:T(8,128)(2,1)} %param.9, bf16[4096,3072]{1,0:T(8,128)(2,1)} %get-tuple-element.9, f32[4096,3072]{1,0:T(8,128)} %get-tuple-element.8, bf16[4096,768]{1,0:T(8,128)(2,1)} %add_convert_fusion, bf16[3072,768]{1,0:T(8,128)(2,1)} %param.12), kind=kOutput, calls=%fused_computation.41 | convolution fusion | flops 38770311168 | bytes 97517568 | tf_op jit(solution)/shard_map/td,tf->df/dot_general | solution.py:36
  282.1 32.6 %convolution_convert_fusion.2 = bf16[3072,768]{1,0:T(8,128)(2,1)} fusion(bf16[4096,768]{1,0:T(8,128)(2,1)} %add_convert_fusion, f32[4096,3072]{1,0:T(8,128)} %get-tuple-element.8, bf16[4096,3072]{1,0:T(8,128)(2,1)} %get-tuple-element.9), kind=kOutput, calls=%fused_computation.39 | convolution fusion | flops 19380043776 | bytes 86507520 | tf_op jit(solution)/shard_map/tf,td->fd/dot_general | solution.py:34
  314.6 8.2 concatenate.13
  322.9 8.1 concatenate.12
  331.0 8.1 concatenate.14
  345.9 8.2 concatenate.15
  354.1 19.0 %pad_maximum_fusion = bf16[4,4,589824]{2,1,0:T(4,128)(2,1)S(1)} fusion(bf16[1,4,589824]{2,1,0:T(4,128)(2,1)} %concatenate.15, bf16[1,4,589824]{2,1,0:T(4,128)(2,1)} %concatenate.14, bf16[1,4,589824]{2,1,0:T(4,128)(2,1)} %concatenate.13, bf16[1,4,589824]{2,1,0:T(4,128)(2,1)} %concatenate.12), kind=kLoop, calls=%fused_computation.33 | loop fusion | flops 28311552 | bytes 37748736 | tf_op jit(solution)/shard_map/concatenate | solution.py:37
  373.1 35.7 %copy.18 = bf16[4,4,589824]{2,0,1:T(4,128)(2,1)} copy(bf16[4,4,589824]{2,1,0:T(4,128)(2,1)S(1)} %pad_maximum_fusion) | data formatting | bytes 37748736 | tf_op jit(solution)/shard_map/concatenate | solution.py:37
  408.7 218.1 %all_to_all.5 = bf16[4,4,589824]{2,0,1:T(4,128)(2,1)} all-to-all(bf16[4,4,589824]{2,0,1:T(4,128)(2,1)} %copy.18), channel_id=1, replica_groups=mesh['dpz'=2,'dpy'=2,'dpx'=4] {'dpx'}, dimensions={1} | all-to-all | bytes 37748736 | tf_op jit(solution)/shard_map/all_to_all | solution.py:49
  626.8 18.8 %convert_reduce_fusion = f32[4,589824]{1,0:T(4,128)} fusion(bf16[4,4,589824]{2,0,1:T(4,128)(2,1)} %all_to_all.5), kind=kLoop, calls=%fused_computation.28 | loop fusion | flops 16515072 | bytes 28311552 | tf_op jit(solution)/shard_map/reduce_sum | solution.py:50
  645.6 21.4 %reshape.27 = f32[2,2,589824]{2,1,0:T(2,128)} reshape(f32[4,589824]{1,0:T(4,128)} %convert_reduce_fusion) | data formatting | bytes 18874368 | tf_op jit(solution)/shard_map/reshape | solution.py:51
  666.9 17.1 %copy.19 = f32[2,2,589824]{2,0,1:T(2,128)} copy(f32[2,2,589824]{2,1,0:T(2,128)} %reshape.27) | data formatting | bytes 18874368 | tf_op jit(solution)/shard_map/reshape | solution.py:51
  685.3 216.5 %all-reduce.5.cloned.1.call-done = f32[2,2,589824]{2,0,1:T(2,128)} async-done(((f32[2,2,589824]{2,0,1:T(2,128)}), f32[2,2,589824]{2,0,1:T(2,128)}) %all-reduce.5.cloned.1.call-update) | async-done | bytes 9437200
  906.4 7.8 copy.20
  914.9 114.7 %all-reduce.7.cloned.1.call-done = f32[2,1,589824]{2,1,0:T(1,128)} async-done(((f32[2,1,589824]{2,1,0:T(1,128)}), f32[2,1,589824]{2,1,0:T(1,128)}) %all-reduce.7.cloned.1.call-update) | async-done | bytes 4718608
  1040.3 83.0 %all-gather.2.cloned.1.call-done = bf16[9437184]{0:T(1024)(128)(2,1)} async-done(((bf16[589824]{0:T(1024)(128)(2,1)}), bf16[9437184]{0:T(1024)(128)(2,1)}) %all-gather.2.cloned.1.call-update) | async-done | bytes 18874384 | tf_op jit(solution)/shard_map/all_gather | solution.py:59
  1123.2 16.4 %copy.24 = bf16[9437184]{0:T(1024)(128)(2,1)} copy(bf16[9437184]{0:T(1024)(128)(2,1)} %all-gather.2.cloned.1.call-done) | data formatting | bytes 37748736
  (30 shorter events, 23.9 us)
Async XLA Ops:
  7.2 894.6 %all-reduce.5.cloned.1.call-start = ((), (), s32[]{:S(2)}) async-start(), calls=%async_computation.2 | async-start | bytes 18874368
  40.6 87.8 %slice-start = ((s8[4718592]{0:T(1024)(128)(4,1)}), s8[524288]{0:T(1024)(128)(4,1)S(1)}, s32[]{:S(2)}) async-start(s8[4718592]{0:T(1024)(128)(4,1)} %bitcast.28), calls=%async_computation.4 | async-start | bytes 1048576
  75.9 27.1 %copy-start.1 = (bf16[4096,768]{1,0:T(8,128)(2,1)S(1)}, bf16[4096,768]{1,0:T(8,128)(2,1)}, u32[]{:S(2)}) copy-start(bf16[4096,768]{1,0:T(8,128)(2,1)} %param.10) | copy-start | bytes 18874372
  75.9 52.5 %slice-start.1 = ((s8[4718592]{0:T(1024)(128)(4,1)}), s8[4194304]{0:T(1024)(128)(4,1)S(1)}, s32[]{:S(2)}) async-start(s8[4718592]{0:T(1024)(128)(4,1)} %bitcast.28), calls=%async_computation.5 | async-start | bytes 8388608
  103.0 63.0 %slice-start.2 = ((s8[6291456]{0:T(1024)(128)(4,1)}), s8[4194304]{0:T(1024)(128)(4,1)S(1)}, s32[]{:S(2)}) async-start(s8[6291456]{0:T(1024)(128)(4,1)} %bitcast.30), calls=%async_computation.6 | async-start | bytes 8388608
  128.4 37.6 %slice-start.3 = ((s8[6291456]{0:T(1024)(128)(4,1)}), s8[2097152]{0:T(1024)(128)(4,1)S(1)}, s32[]{:S(2)}) async-start(s8[6291456]{0:T(1024)(128)(4,1)} %bitcast.30), calls=%async_computation.7 | async-start | bytes 4194304
  684.0 0.7 copy-start.3
  684.1 345.5 %all-reduce.7.cloned.1.call-start = ((), (), s32[]{:S(2)}) async-start(), calls=%async_computation.3 | async-start | bytes 9437184
  906.4 7.9 copy-start.2
  906.4 127.2 %copy-start = (f32[589824]{0:T(1024)S(1)}, f32[589824]{0:T(1024)}, u32[]{:S(2)}) copy-start(f32[589824]{0:T(1024)} %param.15) | copy-start | bytes 7077892
  914.2 209.0 %all-gather.2.cloned.1.call-start = ((), (), s32[]{:S(2)}) async-start(), calls=%async_computation.1 | async-start | bytes 20054016 | tf_op jit(solution)/shard_map/all_gather | solution.py:59
Sparse Core Ops, SparseCore 0:
  684.2 217.5 all-reduce.4
  914.4 115.2 all-reduce.6
  1040.4 82.7 all-gather.1
where the time goes:
time: 1150 us
  waiting for transfers between devices  414 us (36%)
  matrix products  307 us (27%)
  blocking collectives  218 us (19%)
  local copies, waits for them, and re-layouts  148 us (13%)
  other arithmetic  44.4 us (4%)
  between operations  14 us (1%)
    unnamed x5, waiting for transfers between devices  331 us
    all_to_all x1, blocking collectives, local_step(): received = lax.all_to_all(grad_grid, 'dpx', 1, 1, tiled=True)  218 us
    all_gather x1, waiting for transfers between devices, local_step(): lax.all_gather(new_master.astype(jnp.bfloat16), AXES, tiled=True)  83 us
    concatenate x5, local copies, waits for them, and re-layouts, device_grads(): jnp.concatenate([g2_out.reshape(-1), g2_in.reshape(-1), g1_out.reshape(-1...  68.3 us
    dot_general x1, matrix products, device_grads(): jnp.einsum('td,tf->df', x_one, dz_one, preferred_element_type=jnp.float32)  65.4 us
    reshape x2, local copies, waits for them, and re-layouts, local_step(): part_x.reshape(size_z, size_y, shard_len)  38.5 us
    dot_general x1, matrix products, device_grads(): jnp.einsum('td,fd->tf', dy_one, w2_out, preferred_element_type=jnp.float32)  37.6 us
    dot_general x1, matrix products, device_grads(): jnp.dot(h_one, w1_out, preferred_element_type=jnp.float32)  35.3 us
  transfers between devices with their start and end apart: 3, of which 3 were waited for; matrix products, arithmetic and copies ran while one was open for 0% of the time, Pallas kernels for 0%

commit v1 on v0

v1 whole, which is shorter than its diff:
```python
import math
import jax
import jax.numpy as jnp
from jax import lax
from jax.experimental import pallas as pl
from jax.experimental.pallas import tpu as pltpu
from jax.sharding import PartitionSpec as P

AXES = ('dpz', 'dpy', 'dpx')
STEP = 10
BETA_ONE = 0.9
BETA_TWO = 0.999
LEARN_RATE = 0.001
ADAM_EPS = 1e-8


def gelu_value(z_val):
    return 0.5 * z_val * (1.0 + lax.erf(z_val * (1.0 / math.sqrt(2.0))))


def gelu_slope(z_val):
    cdf_part = 0.5 * (1.0 + lax.erf(z_val * (1.0 / math.sqrt(2.0))))
    return cdf_part + z_val * jnp.exp(-0.5 * z_val * z_val) * (1.0 / math.sqrt(2.0 * math.pi))


def dev(z, y, x):
    return (z * 2 + y) * 4 + x


def send_x(blocks, x_idx):
    own = lax.dynamic_index_in_dim(blocks, x_idx, 0, keepdims=False)
    got = [own]
    for k in (2, 3, 1):
        send = lax.dynamic_index_in_dim(blocks, x_idx ^ k, 0, keepdims=False)
        got.append(lax.ppermute(send, 'dpx', [(i, i ^ k) for i in range(4)]))
    return got


def add_x(got):
    total = got[3].astype(jnp.float32) + got[0].astype(jnp.float32)
    return total + (got[1].astype(jnp.float32) + got[2].astype(jnp.float32))


def shift_z(val, y_rel, zo, yo):
    pairs = [(dev(1 - zo, yo ^ ry, x), dev(zo, yo ^ ry, x)) for ry in y_rel for x in range(4)]
    return lax.ppermute(val, AXES, pairs)


def shift_y(val, z_rel, zo, yo):
    pairs = [(dev(zo ^ rz, 1 - yo, x), dev(zo ^ rz, yo, x)) for rz in z_rel for x in range(4)]
    return lax.ppermute(val, AXES, pairs)


def send_one(part, zo, yo):
    half = part.shape[0] // 2
    a_part, b_part = part[:half], part[half:]
    return a_part, b_part, shift_z(a_part, (0, 1), zo, yo), shift_y(b_part, (0, 1), zo, yo)


def add_one(sent):
    return sent[0] + sent[2], sent[1] + sent[3]


def send_two(halves, zo, yo):
    return halves[0], halves[1], shift_y(halves[0], (0,), zo, yo), shift_z(halves[1], (0,), zo, yo)


def add_two(sent):
    return jnp.concatenate([sent[0] + sent[2], sent[1] + sent[3]], axis=0)


def after(val, *deps):
    out = lax.optimization_barrier((val,) + deps)
    return out[0], out[1:]


SHARD_ROWS = 4608
N_PIECE = 6
PIECE_ROWS = SHARD_ROWS // N_PIECE
CH_COLS = 512
N_CH = 6
N_PRE = 4
PRE_COLS = N_PRE * CH_COLS
REST_COLS = 3072 - PRE_COLS
X_BIT, Y_BIT, Z_BIT = 1, 2, 4
ADAM_ROWS = 96
ORDERS = ((X_BIT, Y_BIT, Z_BIT), (Y_BIT, Z_BIT, X_BIT), (Z_BIT, X_BIT, Y_BIT)) * 2


def tail_kernel(p_hbm, gd_hbm, s_hbm, mst_hbm, m_hbm, v_hbm,
                omst_hbm, om_hbm, ov_hbm, w_hbm,
                own, xrecv, part, a1, b1, a2, b2, s_v, mst_v, m_v, v_v, w_v,
                ld_sem, st_sem, xs_send, xs_recv, yz_send, yz_recv, ag_send, ag_recv, dd_send, dd_recv):
    z, y, x = (lax.axis_index(a) for a in AXES)
    ny, nz = 1 - y, 1 - z
    is_late = (z == 1) & (y == 1)
    f32 = jnp.float32

    def x_peer(k):
        if k == 2:
            return lax.rem(x + 2, 4)
        flip = x + 1 - 2 * lax.rem(x, 2)
        return flip if k == 1 else lax.rem(flip + 2, 4)

    peers = {X_BIT: {'dpx': x_peer(2)}, Y_BIT: {'dpy': ny}, Z_BIT: {'dpz': nz}}

    barrier = pltpu.get_barrier_semaphore()
    for where in ({'dpx': x_peer(1)}, {'dpx': x_peer(2)}, {'dpx': x_peer(3)}, {'dpy': ny}, {'dpz': nz}):
        pl.semaphore_signal(barrier, inc=1, device_id=where, device_id_type=pl.DeviceIdType.MESH)
    pl.semaphore_wait(barrier, 5)

    def remote(src, dst, send, recv, where):
        return pltpu.make_async_remote_copy(src_ref=src, dst_ref=dst, send_sem=send, recv_sem=recv,
                                            device_id=where, device_id_type=pl.DeviceIdType.MESH)

    def xs_copy(k, ch):
        lo = (ch - N_PRE) * CH_COLS
        to = x_peer(k)
        return remote(gd_hbm.at[pl.ds(to * 192, 192), pl.ds(lo, CH_COLS)],
                      xrecv.at[k - 1, :, pl.ds(lo, CH_COLS)],
                      xs_send.at[k - 1, ch - N_PRE], xs_recv.at[k - 1, ch - N_PRE], {'dpx': to})

    for ch in range(N_PRE, N_CH):
        for k in (2, 3, 1):
            xs_copy(k, ch).start()

    loads = [pltpu.make_async_copy(p_hbm, part.at[:, pl.ds(0, PRE_COLS)], ld_sem.at[0]),
             pltpu.make_async_copy(gd_hbm.at[pl.ds(x * 192, 192), :], own, ld_sem.at[1]),
             pltpu.make_async_copy(mst_hbm, mst_v, ld_sem.at[2]),
             pltpu.make_async_copy(m_hbm, m_v, ld_sem.at[3]),
             pltpu.make_async_copy(v_hbm, v_v, ld_sem.at[4])]
    for cp in loads:
        cp.start()
    load_s = pltpu.make_async_copy(s_hbm, s_v, ld_sem.at[5])

    @pl.when(jnp.logical_not(is_late))
    def _():
        load_s.start()

    loads[0].wait()

    def cols(ch):
        return pl.ds(ch * CH_COLS, CH_COLS)

    top, bot = pl.ds(0, 96), pl.ds(96, 96)

    def yz_copy(kind, ch):
        rows, dst, where = ((top, a1, peers[Z_BIT]), (bot, b1, peers[Y_BIT]),
                            (top, a2, peers[Y_BIT]), (bot, b2, peers[Z_BIT]))[kind]
        return remote(part.at[rows, cols(ch)], dst.at[:, cols(ch)],
                      yz_send.at[kind, ch], yz_recv.at[kind, ch], where)

    yz_sends = {0: z == 0, 1: y == 0, 2: (z == 1) & (y == 0), 3: (z == 0) & (y == 1)}
    yz_takes = {0: z == 1, 1: y == 1, 2: is_late, 3: is_late}

    def yz_start(kind, ch):
        @pl.when(yz_sends[kind])
        def _():
            yz_copy(kind, ch).start()

    def yz_take(kind, ch):
        @pl.when(yz_takes[kind])
        def _():
            yz_copy(kind, ch).wait_recv()
            got = (a1, b1, a2, b2)[kind]
            base = 0 if kind in (0, 2) else 96

            def body(i, _):
                rows = pl.ds(pl.multiple_of(base + i * 8, 8), 8)
                part[rows, cols(ch)] += got[pl.ds(pl.multiple_of(i * 8, 8), 8), cols(ch)]
                return 0

            lax.fori_loop(0, 12, body, 0)

    def x_sum(ch):
        lo = (ch - N_PRE) * CH_COLS
        for k in (2, 3, 1):
            xs_copy(k, ch).wait_recv()

        def body(i, _):
            rows = pl.ds(pl.multiple_of(i * 16, 16), 16)
            cc = pl.ds(lo, CH_COLS)
            part[rows, cols(ch)] = ((own[rows, cc].astype(f32) + xrecv[0, rows, cc].astype(f32))
                                    + (xrecv[1, rows, cc].astype(f32) + xrecv[2, rows, cc].astype(f32)))
            return 0

        lax.fori_loop(0, 12, body, 0)

    def adam():
        def body(i, _):
            rows = pl.ds(pl.multiple_of(i * ADAM_ROWS, ADAM_ROWS), ADAM_ROWS)
            g_sum = s_v[rows, :]
            new_m = BETA_ONE * m_v[rows, :] + (1.0 - BETA_ONE) * g_sum
            new_v = BETA_TWO * v_v[rows, :] + (1.0 - BETA_TWO) * g_sum * g_sum
            m_hat = new_m / (1.0 - BETA_ONE ** STEP)
            v_hat = new_v / (1.0 - BETA_TWO ** STEP)
            new_w = mst_v[rows, :] - LEARN_RATE * m_hat / (jnp.sqrt(v_hat) + ADAM_EPS)
            m_v[rows, :] = new_m
            v_v[rows, :] = new_v
            mst_v[rows, :] = new_w
            w_v[rows, :] = new_w.astype(jnp.bfloat16)
            return 0

        lax.fori_loop(0, SHARD_ROWS // ADAM_ROWS, body, 0)

    def shard_rows(h, r):
        zz = nz if r & Z_BIT else z
        yy = ny if r & Y_BIT else y
        xx = x_peer(2) if r & X_BIT else x
        return pl.ds(pl.multiple_of(((zz * 2 + yy) * 4 + xx) * SHARD_ROWS + h * PIECE_ROWS, 256), PIECE_ROWS)

    def ag_copy(h, r, bit):
        rows = shard_rows(h, r)
        return remote(w_hbm.at[rows, :], w_hbm.at[rows, :], ag_send.at[h, bit.bit_length() - 1, r],
                      ag_recv.at[h, r ^ bit], peers[bit])

    def ag_arrived(h, r):
        rows = shard_rows(h, r)
        bit = ORDERS[h][max(i for i in range(3) if r & ORDERS[h][i])]
        remote(w_hbm.at[rows, :], w_hbm.at[rows, :], ag_send.at[h, 0, r], ag_recv.at[h, r], peers[bit]).wait_recv()

    def dd_copy(h, r):
        rows = shard_rows(h, r)
        return remote(w_hbm.at[rows, :], w_hbm.at[rows, :], dd_send.at[h, r], dd_recv.at[h, r], {'dpx': x_peer(1)})

    def next_bits(h, r):
        last = max([i for i in range(3) if r & ORDERS[h][i]], default=-1)
        return ORDERS[h][last + 1:]

    def hops(step):
        for sub in range(1 << step):
            for h in range(N_PIECE):
                o = ORDERS[h]
                r = o[step] | (o[0] if sub & 1 else 0) | (o[1] if sub & 2 else 0)
                ag_arrived(h, r)
                for bit in next_bits(h, r):
                    ag_copy(h, r, bit).start()
                dd_copy(h, r).start()

    outs = [pltpu.make_async_copy(mst_v, omst_hbm, st_sem.at[0]),
            pltpu.make_async_copy(m_v, om_hbm, st_sem.at[1]),
            pltpu.make_async_copy(v_v, ov_hbm, st_sem.at[2])]

    def own_update():
        adam()
        mine = shard_rows(0, 0)
        rows = pl.ds(mine.start, SHARD_ROWS)
        put = pltpu.make_async_copy(w_v, w_hbm.at[rows, :], st_sem.at[3])
        put.start()
        for cp in outs:
            cp.start()
        put.wait()

    for ch in range(N_PRE):
        yz_start(0, ch)
        yz_start(1, ch)
    for cp in loads[1:]:
        cp.wait()

    @pl.when(jnp.logical_not(is_late))
    def _():
        load_s.wait()
        own_update()

    for ch in range(N_PRE):
        yz_take(0, ch)
        yz_take(1, ch)
        yz_start(2, ch)
        yz_start(3, ch)
    for ch in range(N_PRE, N_CH):
        x_sum(ch)
        yz_start(0, ch)
        yz_start(1, ch)
    for ch in range(N_PRE, N_CH):
        yz_take(0, ch)
        yz_take(1, ch)
        yz_start(2, ch)
        yz_start(3, ch)

    @pl.when(is_late)
    def _():
        for ch in range(N_CH):
            for kind in (2, 3):
                yz_take(kind, ch)

        def body(g, _):
            rows = pl.ds(pl.multiple_of(g * 8, 8), 8)
            for j in range(24):
                s_v[pl.ds(g * 192 + j, 8, stride=24), :] = part[rows, 128 * j:128 * (j + 1)]
            return 0

        lax.fori_loop(0, 24, body, 0)
        own_update()

    for step in range(3):
        for h in range(N_PIECE):
            ag_copy(h, 0, ORDERS[h][step]).start()
    for h in range(N_PIECE):
        dd_copy(h, 0).start()
    for step in range(3):
        hops(step)

    for h in range(N_PIECE):
        for r in range(8):
            for bit in next_bits(h, r):
                ag_copy(h, r, bit).wait_send()
            dd_copy(h, r).wait()
    for ch in range(N_PRE, N_CH):
        for k in (1, 2, 3):
            xs_copy(k, ch).wait_send()
    for ch in range(N_CH):
        for kind in range(4):
            @pl.when(yz_sends[kind])
            def _():
                yz_copy(kind, ch).wait_send()
    for cp in outs:
        cp.wait()


def tail(p_d0, g_d1, s_abc, master, adam_m, adam_v):
    any_spec = pl.BlockSpec(memory_space=pl.ANY)
    f32, bf16 = jnp.float32, jnp.bfloat16
    dma = pltpu.SemaphoreType.DMA
    shard = jax.ShapeDtypeStruct((SHARD_ROWS, 128), f32)
    state = pltpu.VMEM((SHARD_ROWS, 128), f32)
    return pl.pallas_call(
        tail_kernel,
        out_shape=(shard, shard, shard, jax.ShapeDtypeStruct((16 * SHARD_ROWS, 128), bf16)),
        in_specs=[any_spec] * 6,
        out_specs=[any_spec] * 4,
        scratch_shapes=[
            pltpu.VMEM((192, REST_COLS), bf16), pltpu.VMEM((3, 192, REST_COLS), bf16), pltpu.VMEM((192, 3072), f32),
            pltpu.VMEM((96, 3072), f32), pltpu.VMEM((96, 3072), f32), pltpu.VMEM((96, 3072), f32),
            pltpu.VMEM((96, 3072), f32), state, state, state, state, pltpu.VMEM((SHARD_ROWS, 128), bf16),
            dma((6,)), dma((4,)), dma((3, N_CH - N_PRE)), dma((3, N_CH - N_PRE)), dma((4, N_CH)), dma((4, N_CH)),
            dma((6, 3, 8)), dma((6, 8)), dma((6, 8)), dma((6, 8)),
        ],
        compiler_params=pltpu.CompilerParams(collective_id=0, has_side_effects=True, vmem_limit_bytes=48 << 20),
        name="tail",
    )(p_d0, g_d1, s_abc, master, adam_m, adam_v)


def solution(mesh):
    def inner_step(x_one, dy_one, w1_in, w1_out, w2_in, w2_out, master, adam_m, adam_v):
        zi, yi, xi = (lax.axis_index(a) for a in AXES)
        f32, bf16 = jnp.float32, jnp.bfloat16

        def mm(spec, a, b):
            return jnp.einsum(spec, a, b, preferred_element_type=f32)

        z_one = mm('td,df->tf', x_one, w1_in).astype(bf16)
        h_one = gelu_value(z_one.astype(f32)).astype(bf16)
        z_one, h_one = lax.optimization_barrier((z_one, h_one))
        x_two = (x_one.astype(f32) + mm('tf,fd->td', h_one, w1_out)).astype(bf16)
        z_two = mm('td,df->tf', x_two, w2_in).astype(bf16)
        h_two = gelu_value(z_two.astype(f32)).astype(bf16)
        z_two, h_two = lax.optimization_barrier((z_two, h_two))
        g_a = mm('tf,td->fd', h_two, dy_one).astype(bf16)
        x_a = send_x(g_a.reshape(4, 768, 768), xi)
        dz_two = (mm('td,fd->tf', dy_one, w2_out) * gelu_slope(z_two.astype(f32))).astype(bf16)
        g_b = mm('td,tf->df', x_two, dz_two).astype(bf16)
        x_b = send_x(g_b.reshape(4, 192, 3072), xi)
        p_a = add_x(x_a)
        dz_two, (p_a,) = after(dz_two, p_a)
        one_a = send_one(p_a, 0, 0)
        dx_two = (dy_one.astype(f32) + mm('tf,df->td', dz_two, w2_in)).astype(bf16)
        g_c = mm('tf,td->fd', h_one, dx_two).astype(bf16)
        x_c = send_x(g_c.reshape(4, 768, 768), xi)
        p_b = add_x(x_b)
        q_a = add_one(one_a)
        dx_two, (p_b, qa0, qa1) = after(dx_two, p_b, *q_a)
        two_a = send_two((qa0, qa1), 0, 0)
        one_b = send_one(p_b, 0, 1)

        def slope_grad(lo, hi):
            up = mm('td,fd->tf', dx_two, w1_out[lo:hi])
            return (up * gelu_slope(z_one[:, lo:hi].astype(f32))).astype(bf16)

        dz_pre = slope_grad(0, PRE_COLS)
        s_a = add_two(two_a).reshape(-1)
        q_b = add_one(one_b)
        dz_pre, (qb0, qb1, s_a) = after(dz_pre, *q_b, s_a)
        two_b = send_two((qb0, qb1), 0, 1)
        g_d0 = mm('td,tf->df', x_one, dz_pre).astype(bf16)
        x_d0 = send_x(g_d0.reshape(4, 192, PRE_COLS), xi)
        p_c = add_x(x_c)
        dx_two, (p_c,) = after(dx_two, p_c)
        one_c = send_one(p_c, 1, 0)
        dz_rest = slope_grad(PRE_COLS, 3072)
        s_b = add_two(two_b).reshape(-1)
        q_c = add_one(one_c)
        dz_rest, (qc0, qc1, s_b) = after(dz_rest, *q_c, s_b)
        two_c = send_two((qc0, qc1), 1, 0)
        g_d1 = mm('td,tf->df', x_one, dz_rest).astype(bf16)
        s_c = add_two(two_c).reshape(-1)
        s_abc = jnp.where(zi == 0, jnp.where(yi == 0, s_a, s_b), s_c)
        flat = lambda t: t.reshape(SHARD_ROWS, 128)
        new_master, new_m, new_v, weights = tail(add_x(x_d0), g_d1, flat(s_abc), flat(master), flat(adam_m), flat(adam_v))
        return new_master.reshape(-1), new_m.reshape(-1), new_v.reshape(-1), weights.reshape(-1)

    in_specs = (P(AXES, None), P(AXES, None), P(), P(), P(), P(), P(AXES), P(AXES), P(AXES))
    out_specs = (P(AXES), P(AXES), P(AXES), P())
    return jax.shard_map(inner_step, mesh=mesh, in_specs=in_specs, out_specs=out_specs, check_vma=False)
```

time: 1150 us -> 580 us (0.50)
  the two profiles are of different devices: /device:TPU:0 before, /device:TPU:5 now
where the time goes in v1:
time: 580 us; the launch traced here: 573 us
  matrix products  291 us (50%)
  Pallas kernels  148 us (26%)
  starting transfers between devices  46.6 us (8%)
  local copies, waits for them, and re-layouts  44.8 us (8%)
  waiting for transfers between devices  21.7 us (4%)
  other arithmetic  20.2 us (3%)
    dot_general x12, matrix products, mm(): return jnp.einsum(spec, a, b, preferred_element_type=f32)  291 us
    pallas_call x1, Pallas kernels, tail(): pl.pallas_call(tail_kernel, out_shape=(shard, shard, shard, jax.ShapeDtyp...  148 us
    unnamed x41, local copies, waits for them, and re-layouts  29.2 us
    ppermute x12, waiting for transfers between devices, send_x(): got.append(lax.ppermute(send, 'dpx', [(i, i ^ k) for i in range(4)]))  21.6 us
    ppermute x6, starting transfers between devices, shift_z(): return lax.ppermute(val, AXES, pairs)  21.5 us
    ppermute x6, starting transfers between devices, shift_y(): return lax.ppermute(val, AXES, pairs)  13.5 us
  transfers between devices with their start and end apart: 24, of which 3 were waited for; matrix products, arithmetic and copies ran while one was open for 36% of the time, Pallas kernels for 0%

profile of v1, /device:TPU:5, one launch (start us, length us, event | category | flops | bytes accessed | tf_op | source)
XLA Modules:
  0.0 572.9 jit_solution(14923387886214925427)
XLA Ops:
  0.7 30.4 %fusion.1 = (bf16[4096,3072]{1,0:T(8,128)(2,1)}, bf16[4096,3072]{1,0:T(8,128)(2,1)}) fusion(bf16[4096,768]{1,0:T(8,128)(2,1)} %param.9, bf16[768,3072]{1,0:T(8,128)(2,1)} %param.11), kind=kOutput, calls=%fused_computation.13 | convolution fusion | flops 19415433216 | bytes 61341696 | tf_op jit(solution)/shard_map/td,df->tf/dot_general | solution.py:349
  31.0 24.4 %add_convert_fusion.1 = bf16[4096,768]{1,0:T(8,128)(2,1)} fusion(bf16[4096,768]{1,0:T(8,128)(2,1)S(1)} %copy-done.8, bf16[4096,3072]{1,0:T(8,128)(2,1)} %get-tuple-element.28, bf16[3072,768]{1,0:T(8,128)(2,1)S(1)} %copy-done.9), kind=kOutput, calls=%fused_computation.51 | convolution fusion | flops 19336790016 | bytes 42467328 | tf_op jit(solution)/shard_map/tf,fd->td/dot_general | solution.py:349
  55.5 29.4 %fusion.5 = (bf16[4096,3072]{1,0:T(8,128)(2,1)}, bf16[4096,3072]{1,0:T(8,128)(2,1)}) fusion(bf16[4096,768]{1,0:T(8,128)(2,1)} %add_convert_fusion.1, bf16[768,3072]{1,0:T(8,128)(2,1)S(1)} %bitcast.97), kind=kOutput, calls=%fused_computation.17 | convolution fusion | flops 19415433216 | bytes 61341696 | tf_op jit(solution)/shard_map/td,df->tf/dot_general | solution.py:349
  84.8 25.3 %convolution_convert_fusion.4 = bf16[3072,768]{1,0:T(8,128)(2,1)S(1)} fusion(bf16[4096,3072]{1,0:T(8,128)(2,1)} %get-tuple-element.30, bf16[4096,768]{1,0:T(8,128)(2,1)} %param.10), kind=kOutput, calls=%fused_computation.54 | convolution fusion | flops 19329712128 | bytes 36175872 | tf_op jit(solution)/shard_map/tf,td->fd/dot_general | solution.py:349
  116.5 38.3 %fusion.15 = bf16[4096,3072]{1,0:T(8,128)(2,1)} fusion(bf16[4096,3072]{1,0:T(8,128)(2,1)} %get-tuple-element.29, bf16[4096,768]{1,0:T(8,128)(2,1)} %param.10, bf16[3072,768]{1,0:T(8,128)(2,1)} %param.14), kind=kOutput, calls=%fused_computation.27 | convolution fusion | flops 19465764864 | bytes 61341696 | tf_op jit(solution)/shard_map/td,fd->tf/dot_general | solution.py:349
  154.7 23.9 %convolution_convert_fusion.3 = bf16[768,3072]{1,0:T(8,128)(2,1)S(1)} fusion(bf16[4096,768]{1,0:T(8,128)(2,1)S(1)} %bitcast.101, bf16[4096,3072]{1,0:T(8,128)(2,1)} %fusion.15), kind=kOutput, calls=%fused_computation.53 | convolution fusion | flops 19329712128 | bytes 36175872 | tf_op jit(solution)/shard_map/td,tf->df/dot_general | solution.py:349
  184.9 2.5 fusion.35
  190.3 2.7 collective-permute-start.7
  193.0 27.3 %add_convert_fusion = bf16[4096,768]{1,0:T(8,128)(2,1)} fusion(bf16[4096,768]{1,0:T(8,128)(2,1)} %param.10, bf16[4096,3072]{1,0:T(8,128)(2,1)} %fusion.15, bf16[768,3072]{1,0:T(8,128)(2,1)} %param.13), kind=kOutput, calls=%fused_computation.50 | convolution fusion | flops 19336790016 | bytes 42467328 | tf_op jit(solution)/shard_map/tf,df->td/dot_general | solution.py:349
  220.3 25.2 %convolution_convert_fusion.2 = bf16[3072,768]{1,0:T(8,128)(2,1)S(1)} fusion(bf16[4096,3072]{1,0:T(8,128)(2,1)} %get-tuple-element.28, bf16[4096,768]{1,0:T(8,128)(2,1)} %add_convert_fusion), kind=kOutput, calls=%fused_computation.52 | convolution fusion | flops 19329712128 | bytes 36175872 | tf_op jit(solution)/shard_map/tf,td->fd/dot_general | solution.py:349
  255.7 12.3 %collective-permute-start.11 = (f32[384,768]{1,0:T(8,128)S(1)}, f32[384,768]{1,0:T(8,128)S(1)}, u32[]{:S(2)}, u32[]{:S(2)}) collective-permute-start(f32[384,768]{1,0:T(8,128)S(1)} %get-tuple-element.37), channel_id=1, source_target_pairs={{8,0},{9,1},{10,2},{11,3}} | collective-permute-start | bytes 3538952 | tf_op jit(solution)/shard_map/ppermute | solution.py:46
  270.9 3.0 collective-permute-done.16
  275.2 26.5 %fusion.23 = bf16[4096,2048]{1,0:T(8,128)(2,1)} fusion(bf16[4096,768]{1,0:T(8,128)(2,1)} %add_convert_fusion, bf16[4096,3072]{1,0:T(8,128)(2,1)} %get-tuple-element.34, bf16[3072,768]{1,0:T(8,128)(2,1)S(1)} %bitcast.99), kind=kOutput, calls=%fused_computation.35 | convolution fusion | flops 12977176576 | bytes 42991616 | tf_op jit(solution)/shard_map/td,fd->tf/dot_general | solution.py:349
  303.9 4.4 collective-permute-start.18
  308.3 6.0 %collective-permute-start.19 = (f32[384,768]{1,0:T(8,128)}, f32[384,768]{1,0:T(8,128)}, u32[]{:S(2)}, u32[]{:S(2)}) collective-permute-start(f32[384,768]{1,0:T(8,128)} %get-tuple-element.66), channel_id=1, source_target_pairs={{12,8},{13,9},{14,10},{15,11},{4,0},{5,1},{6,2},{7,3}} | collective-permute-start | bytes 3538952 | tf_op jit(solution)/shard_map/ppermute | solution.py:51
  316.2 3.2 reshape.63
  323.9 18.8 %convolution_convert_fusion.5 = bf16[2048,768]{0,1:T(8,128)(2,1)S(1)} fusion(bf16[4096,2048]{1,0:T(8,128)(2,1)} %fusion.23, bf16[4096,768]{1,0:T(8,128)(2,1)} %param.9), kind=kOutput, calls=%fused_computation.55 | convolution fusion | flops 12886474752 | bytes 26214400 | tf_op jit(solution)/shard_map/td,tf->df/dot_general | solution.py:349
  347.0 14.2 %fusion.31 = bf16[4096,1024]{1,0:T(8,128)(2,1)S(1)} fusion(bf16[4096,3072]{1,0:T(8,128)(2,1)} %get-tuple-element.34, bf16[4096,768]{1,0:T(8,128)(2,1)} %add_convert_fusion, bf16[3072,768]{1,0:T(8,128)(2,1)} %param.12), kind=kOutput, calls=%fused_computation.49 | convolution fusion | flops 6488588288 | bytes 24641536 | tf_op jit(solution)/shard_map/td,fd->tf/dot_general | solution.py:349
  364.4 17.1 %collective-permute-done.14 = bf16[192,2048]{1,0:T(8,128)(2,1)S(1)} collective-permute-done((bf16[192,2048]{1,0:T(8,128)(2,1)S(1)}, bf16[192,2048]{1,0:T(8,128)(2,1)S(1)}, u32[]{:S(2)}, u32[]{:S(2)}) %collective-permute-start.14) | collective-permute-done | bytes 786464 | tf_op jit(solution)/shard_map/ppermute | solution.py:35
  387.4 7.1 %fusion.38.gd_hbm = bf16[768,1024]{1,0:T(8,128)(2,1)S(1)} fusion(bf16[4096,1024]{1,0:T(8,128)(2,1)S(1)} %fusion.31, bf16[4096,768]{1,0:T(8,128)(2,1)S(1)} %bitcast.95), kind=kOutput, calls=%fused_computation.71 | convolution fusion | flops 6443237376 | bytes 16252928 | tf_op jit(solution)/shard_map/td,tf->df/dot_general | solution.py:349
  396.3 3.2 reshape.67
  399.5 3.4 select_bitcast_fusion.s_hbm
  402.9 147.6 %tail.1 = (f32[4608,128]{1,0:T(8,128)S(1)}, f32[4608,128]{1,0:T(8,128)}, f32[4608,128]{1,0:T(8,128)}, bf16[73728,128]{1,0:T(8,128)(2,1)}) custom-call(f32[192,2048]{1,0:T(8,128)S(1)} %fusion.36.p_hbm, bf16[768,1024]{1,0:T(8,128)(2,1)S(1)} %fusion.38.gd_hbm, f32[4608,128]{1,0:T(8,128)} %select_bitcast_fusion.s_hbm, f32[4608,128]{1,0:T(8,128)} %bitcast.91, ...), custom_call_target="tpu_custom_call" | custom-call | tf_op jit(solution)/shard_map/tail/pallas_call | solution.py:326
  556.2 16.4 %copy.23 = bf16[9437184]{0:T(1024)(128)(2,1)} copy(bf16[9437184]{0:T(1024)(128)(2,1)} %bitcast.79) | data formatting | bytes 37748736
  (108 shorter events, 58.9 us)
Async XLA Ops:
  114.1 70.4 %collective-permute-start = (bf16[768,768]{1,0:T(8,128)(2,1)}, bf16[768,768]{1,0:T(8,128)(2,1)S(1)}, u32[]{:S(2)}, u32[]{:S(2)}) collective-permute-start(bf16[768,768]{1,0:T(8,128)(2,1)} %get-tuple-element.58), channel_id=1, source_target_pairs={{0,1},{1,0},{2,3},{3,2},{4,5},{5,4},{6,7},{7,6},{8,9},{9,8},{10,11... | collective-permute-start | bytes 3538952 | tf_op jit(solution)/shard_map/ppermute | solution.py:35
  114.8 70.1 %collective-permute-start.1 = (bf16[768,768]{1,0:T(8,128)(2,1)}, bf16[768,768]{1,0:T(8,128)(2,1)}, u32[]{:S(2)}, u32[]{:S(2)}) collective-permute-start(bf16[768,768]{1,0:T(8,128)(2,1)} %get-tuple-element.60), channel_id=1, source_target_pairs={{0,2},{1,3},{2,0},{3,1},{4,6},{5,7},{6,4},{7,5},{8,10},{9,11},{10,... | collective-permute-start | bytes 3538952 | tf_op jit(solution)/shard_map/ppermute | solution.py:35
  116.0 68.9 %collective-permute-start.2 = (bf16[768,768]{1,0:T(8,128)(2,1)}, bf16[768,768]{1,0:T(8,128)(2,1)}, u32[]{:S(2)}, u32[]{:S(2)}) collective-permute-start(bf16[768,768]{1,0:T(8,128)(2,1)} %get-tuple-element.59), channel_id=1, source_target_pairs={{0,3},{1,2},{2,1},{3,0},{4,7},{5,6},{6,5},{7,4},{8,11},{9,10},{10,... | collective-permute-start | bytes 3538952 | tf_op jit(solution)/shard_map/ppermute | solution.py:35
  182.8 63.0 %collective-permute-start.3 = (bf16[192,3072]{1,0:T(8,128)(2,1)}, bf16[192,3072]{1,0:T(8,128)(2,1)S(1)}, u32[]{:S(2)}, u32[]{:S(2)}) collective-permute-start(bf16[192,3072]{1,0:T(8,128)(2,1)} %get-tuple-element.55), channel_id=1, source_target_pairs={{0,1},{1,0},{2,3},{3,2},{4,5},{5,4},{6,7},{7,6},{8,9},{9,8},{10,11... | collective-permute-start | bytes 3538952 | tf_op jit(solution)/shard_map/ppermute | solution.py:35
  183.0 63.5 %collective-permute-start.4 = (bf16[192,3072]{1,0:T(8,128)(2,1)}, bf16[192,3072]{1,0:T(8,128)(2,1)S(1)}, u32[]{:S(2)}, u32[]{:S(2)}) collective-permute-start(bf16[192,3072]{1,0:T(8,128)(2,1)} %get-tuple-element.57), channel_id=1, source_target_pairs={{0,2},{1,3},{2,0},{3,1},{4,6},{5,7},{6,4},{7,5},{8,10},{9,11},{10,... | collective-permute-start | bytes 3538952 | tf_op jit(solution)/shard_map/ppermute | solution.py:35
  184.5 63.0 %collective-permute-start.5 = (bf16[192,3072]{1,0:T(8,128)(2,1)}, bf16[192,3072]{1,0:T(8,128)(2,1)S(1)}, u32[]{:S(2)}, u32[]{:S(2)}) collective-permute-start(bf16[192,3072]{1,0:T(8,128)(2,1)} %get-tuple-element.56), channel_id=1, source_target_pairs={{0,3},{1,2},{2,1},{3,0},{4,7},{5,6},{6,5},{7,4},{8,11},{9,10},{10,... | collective-permute-start | bytes 3538952 | tf_op jit(solution)/shard_map/ppermute | solution.py:35
  189.0 62.4 %collective-permute-start.6 = (f32[384,768]{1,0:T(8,128)}, f32[384,768]{1,0:T(8,128)S(1)}, u32[]{:S(2)}, u32[]{:S(2)}) collective-permute-start(f32[384,768]{1,0:T(8,128)} %get-tuple-element.75), channel_id=1, source_target_pairs={{8,0},{9,1},{10,2},{11,3},{12,4},{13,5},{14,6},{15,7}} | collective-permute-start | bytes 3538952 | tf_op jit(solution)/shard_map/ppermute | solution.py:46
  190.3 62.2 %collective-permute-start.7 = (f32[384,768]{1,0:T(8,128)}, f32[384,768]{1,0:T(8,128)}, u32[]{:S(2)}, u32[]{:S(2)}) collective-permute-start(f32[384,768]{1,0:T(8,128)} %get-tuple-element.74), channel_id=1, source_target_pairs={{4,0},{5,1},{6,2},{7,3},{12,8},{13,9},{14,10},{15,11}} | collective-permute-start | bytes 3538952 | tf_op jit(solution)/shard_map/ppermute | solution.py:51
  245.7 23.9 %collective-permute-start.15 = (bf16[768,768]{1,0:T(8,128)(2,1)S(1)}, bf16[768,768]{1,0:T(8,128)(2,1)S(1)}, u32[]{:S(2)}, u32[]{:S(2)}) collective-permute-start(bf16[768,768]{1,0:T(8,128)(2,1)S(1)} %get-tuple-element.52), channel_id=1, source_target_pairs={{0,1},{1,0},{2,3},{3,2},{4,5},{5,4},{6,7},{7,6},{8,9},{9,8},{10,11... | collective-permute-start | bytes 3538952 | tf_op jit(solution)/shard_map/ppermute | solution.py:35
  246.4 27.5 %collective-permute-start.16 = (bf16[768,768]{1,0:T(8,128)(2,1)S(1)}, bf16[768,768]{1,0:T(8,128)(2,1)S(1)}, u32[]{:S(2)}, u32[]{:S(2)}) collective-permute-start(bf16[768,768]{1,0:T(8,128)(2,1)S(1)} %get-tuple-element.54), channel_id=1, source_target_pairs={{0,2},{1,3},{2,0},{3,1},{4,6},{5,7},{6,4},{7,5},{8,10},{9,11},{10,... | collective-permute-start | bytes 3538952 | tf_op jit(solution)/shard_map/ppermute | solution.py:35
  247.5 54.1 %collective-permute-start.17 = (bf16[768,768]{1,0:T(8,128)(2,1)S(1)}, bf16[768,768]{1,0:T(8,128)(2,1)S(1)}, u32[]{:S(2)}, u32[]{:S(2)}) collective-permute-start(bf16[768,768]{1,0:T(8,128)(2,1)S(1)} %get-tuple-element.53), channel_id=1, source_target_pairs={{0,3},{1,2},{2,1},{3,0},{4,7},{5,6},{6,5},{7,4},{8,11},{9,10},{10,... | collective-permute-start | bytes 3538952 | tf_op jit(solution)/shard_map/ppermute | solution.py:35
  254.4 54.0 %collective-permute-start.10 = (f32[384,768]{1,0:T(8,128)S(1)}, f32[384,768]{1,0:T(8,128)S(1)}, u32[]{:S(2)}, u32[]{:S(2)}) collective-permute-start(f32[384,768]{1,0:T(8,128)S(1)} %get-tuple-element.36), channel_id=1, source_target_pairs={{4,0},{5,1},{6,2},{7,3}} | collective-permute-start | bytes 3538952 | tf_op jit(solution)/shard_map/ppermute | solution.py:51
  255.7 58.8 %collective-permute-start.11 = (f32[384,768]{1,0:T(8,128)S(1)}, f32[384,768]{1,0:T(8,128)S(1)}, u32[]{:S(2)}, u32[]{:S(2)}) collective-permute-start(f32[384,768]{1,0:T(8,128)S(1)} %get-tuple-element.37), channel_id=1, source_target_pairs={{8,0},{9,1},{10,2},{11,3}} | collective-permute-start | bytes 3538952 | tf_op jit(solution)/shard_map/ppermute | solution.py:46
  269.6 49.8 %collective-permute-start.8 = (f32[96,3072]{1,0:T(8,128)}, f32[96,3072]{1,0:T(8,128)}, u32[]{:S(2)}, u32[]{:S(2)}) collective-permute-start(f32[96,3072]{1,0:T(8,128)} %get-tuple-element.71), channel_id=1, source_target_pairs={{12,4},{13,5},{14,6},{15,7},{8,0},{9,1},{10,2},{11,3}} | collective-permute-start | bytes 3538952 | tf_op jit(solution)/shard_map/ppermute | solution.py:46
  273.9 45.6 %collective-permute-start.9 = (f32[96,3072]{1,0:T(8,128)}, f32[96,3072]{1,0:T(8,128)}, u32[]{:S(2)}, u32[]{:S(2)}) collective-permute-start(f32[96,3072]{1,0:T(8,128)} %get-tuple-element.70), channel_id=1, source_target_pairs={{0,4},{1,5},{2,6},{3,7},{8,12},{9,13},{10,14},{11,15}} | collective-permute-start | bytes 3538952 | tf_op jit(solution)/shard_map/ppermute | solution.py:51
  303.9 41.4 %collective-permute-start.18 = (f32[384,768]{1,0:T(8,128)}, f32[384,768]{1,0:T(8,128)S(1)}, u32[]{:S(2)}, u32[]{:S(2)}) collective-permute-start(f32[384,768]{1,0:T(8,128)} %get-tuple-element.67), channel_id=1, source_target_pairs={{0,8},{1,9},{2,10},{3,11},{4,12},{5,13},{6,14},{7,15}} | collective-permute-start | bytes 3538952 | tf_op jit(solution)/shard_map/ppermute | solution.py:46
  308.3 38.2 %collective-permute-start.19 = (f32[384,768]{1,0:T(8,128)}, f32[384,768]{1,0:T(8,128)}, u32[]{:S(2)}, u32[]{:S(2)}) collective-permute-start(f32[384,768]{1,0:T(8,128)} %get-tuple-element.66), channel_id=1, source_target_pairs={{12,8},{13,9},{14,10},{15,11},{4,0},{5,1},{6,2},{7,3}} | collective-permute-start | bytes 3538952 | tf_op jit(solution)/shard_map/ppermute | solution.py:51
  321.3 60.6 %collective-permute-start.20 = (f32[96,3072]{1,0:T(8,128)S(1)}, f32[96,3072]{1,0:T(8,128)}, u32[]{:S(2)}, u32[]{:S(2)}) collective-permute-start(f32[96,3072]{1,0:T(8,128)S(1)} %get-tuple-element.41), channel_id=1, source_target_pairs={{0,4},{1,5},{2,6},{3,7}} | collective-permute-start | bytes 3538952 | tf_op jit(solution)/shard_map/ppermute | solution.py:51
  322.6 60.7 %collective-permute-start.21 = (f32[96,3072]{1,0:T(8,128)S(1)}, f32[96,3072]{1,0:T(8,128)S(1)}, u32[]{:S(2)}, u32[]{:S(2)}) collective-permute-start(f32[96,3072]{1,0:T(8,128)S(1)} %get-tuple-element.42), channel_id=1, source_target_pairs={{12,4},{13,5},{14,6},{15,7}} | collective-permute-start | bytes 3538952 | tf_op jit(solution)/shard_map/ppermute | solution.py:46
  343.0 19.8 %collective-permute-start.12 = (bf16[192,2048]{1,0:T(8,128)(2,1)S(1)}, bf16[192,2048]{1,0:T(8,128)(2,1)S(1)}, u32[]{:S(2)}, u32[]{:S(2)}) collective-permute-start(bf16[192,2048]{1,0:T(8,128)(2,1)S(1)} %get-tuple-element.61), channel_id=1, source_target_pairs={{0,1},{1,0},{2,3},{3,2},{4,5},{5,4},{6,7},{7,6},{8,9},{9,8},{10,11... | collective-permute-start | bytes 2359304 | tf_op jit(solution)/shard_map/ppermute | solution.py:35
  345.4 19.0 %collective-permute-start.13 = (bf16[192,2048]{1,0:T(8,128)(2,1)S(1)}, bf16[192,2048]{1,0:T(8,128)(2,1)S(1)}, u32[]{:S(2)}, u32[]{:S(2)}) collective-permute-start(bf16[192,2048]{1,0:T(8,128)(2,1)S(1)} %get-tuple-element.63), channel_id=1, source_target_pairs={{0,2},{1,3},{2,0},{3,1},{4,6},{5,7},{6,4},{7,5},{8,10},{9,11},{10,... | collective-permute-start | bytes 2359304 | tf_op jit(solution)/shard_map/ppermute | solution.py:35
  346.6 34.9 %collective-permute-start.14 = (bf16[192,2048]{1,0:T(8,128)(2,1)S(1)}, bf16[192,2048]{1,0:T(8,128)(2,1)S(1)}, u32[]{:S(2)}, u32[]{:S(2)}) collective-permute-start(bf16[192,2048]{1,0:T(8,128)(2,1)S(1)} %get-tuple-element.62), channel_id=1, source_target_pairs={{0,3},{1,2},{2,1},{3,0},{4,7},{5,6},{6,5},{7,4},{8,11},{9,10},{10,... | collective-permute-start | bytes 2359304 | tf_op jit(solution)/shard_map/ppermute | solution.py:35
  385.5 8.9 %collective-permute-start.22 = (f32[384,768]{1,0:T(8,128)S(1)}, f32[384,768]{1,0:T(8,128)S(1)}, u32[]{:S(2)}, u32[]{:S(2)}) collective-permute-start(f32[384,768]{1,0:T(8,128)S(1)} %get-tuple-element.46), channel_id=1, source_target_pairs={{12,8},{13,9},{14,10},{15,11}} | collective-permute-start | bytes 3538952 | tf_op jit(solution)/shard_map/ppermute | solution.py:51
  386.4 8.2 %collective-permute-start.23 = (f32[384,768]{1,0:T(8,128)S(1)}, f32[384,768]{1,0:T(8,128)S(1)}, u32[]{:S(2)}, u32[]{:S(2)}) collective-permute-start(f32[384,768]{1,0:T(8,128)S(1)} %get-tuple-element.47), channel_id=1, source_target_pairs={{0,8},{1,9},{2,10},{3,11}} | collective-permute-start | bytes 3538952 | tf_op jit(solution)/shard_map/ppermute | solution.py:46
  (18 other events, 315.4 us)

commit v2 on v1

--- a/solution.py
+++ b/solution.py
@@ -51,8 +51,8 @@
     return lax.ppermute(val, AXES, pairs)
 
 
-def send_one(part, zo, yo):
-    half = part.shape[0] // 2
+def send_one(part, zo, yo, cut=None):
+    half = cut or part.shape[0] // 2
     a_part, b_part = part[:half], part[half:]
     return a_part, b_part, shift_z(a_part, (0, 1), zo, yo), shift_y(b_part, (0, 1), zo, yo)
 
@@ -63,10 +63,6 @@
 
 def send_two(halves, zo, yo):
     return halves[0], halves[1], shift_y(halves[0], (0,), zo, yo), shift_z(halves[1], (0,), zo, yo)
-
-
-def add_two(sent):
-    return jnp.concatenate([sent[0] + sent[2], sent[1] + sent[3]], axis=0)
 
 
 def after(val, *deps):
@@ -79,18 +75,19 @@
 PIECE_ROWS = SHARD_ROWS // N_PIECE
 CH_COLS = 512
 N_CH = 6
-N_PRE = 4
+N_PRE = 3
 PRE_COLS = N_PRE * CH_COLS
 REST_COLS = 3072 - PRE_COLS
 X_BIT, Y_BIT, Z_BIT = 1, 2, 4
 ADAM_ROWS = 96
+C_TOP = 576
 ORDERS = ((X_BIT, Y_BIT, Z_BIT), (Y_BIT, Z_BIT, X_BIT), (Z_BIT, X_BIT, Y_BIT)) * 2
 
 
-def tail_kernel(p_hbm, gd_hbm, s_hbm, mst_hbm, m_hbm, v_hbm,
-                omst_hbm, om_hbm, ov_hbm, w_hbm,
-                own, xrecv, part, a1, b1, a2, b2, s_v, mst_v, m_v, v_v, w_v,
-                ld_sem, st_sem, xs_send, xs_recv, yz_send, yz_recv, ag_send, ag_recv, dd_send, dd_recv):
+def tail_kernel(p_hbm, gd_hbm, qa_hbm, ra_hbm, qb0_hbm, qb1_hbm, rb0_hbm, rb1_hbm, qc0_hbm, qc1_hbm,
+                mst_hbm, m_hbm, v_hbm, omst_hbm, om_hbm, ov_hbm, w_hbm,
+                own, xrecv, part, a1, b1, a2, b2, sq_a, sq_b, wide_a, wide_b, s_v, mst_v, m_v, v_v, w_v,
+                ld_sem, st_sem, c_send, c_recv, xs_send, xs_recv, yz_send, yz_recv, ag_send, ag_recv, dd_send, dd_recv):
     z, y, x = (lax.axis_index(a) for a in AXES)
     ny, nz = 1 - y, 1 - z
     is_late = (z == 1) & (y == 1)
@@ -131,11 +128,42 @@
              pltpu.make_async_copy(v_hbm, v_v, ld_sem.at[4])]
     for cp in loads:
         cp.start()
-    load_s = pltpu.make_async_copy(s_hbm, s_v, ld_sem.at[5])
-
-    @pl.when(jnp.logical_not(is_late))
-    def _():
-        load_s.start()
+    is_a, is_b, is_c = (z == 0) & (y == 0), (z == 0) & (y == 1), (z == 1) & (y == 0)
+
+    def fetch(items):
+        return [pltpu.make_async_copy(src, dst, ld_sem.at[5 + i]) for i, (src, dst) in enumerate(items)]
+
+    top_c, bot_c = pl.ds(0, C_TOP), pl.ds(C_TOP, 768 - C_TOP)
+    role_loads = {
+        'a': (is_a, fetch([(qa_hbm, sq_a), (ra_hbm, sq_b)])),
+        'b': (is_b, fetch([(qb0_hbm, wide_a.at[pl.ds(0, 96), :]), (qb1_hbm, wide_a.at[pl.ds(96, 96), :]),
+                           (rb0_hbm, wide_b.at[pl.ds(0, 96), :]), (rb1_hbm, wide_b.at[pl.ds(96, 96), :])])),
+        'c': (is_c, fetch([(qc0_hbm, sq_a.at[top_c, :]), (qc1_hbm, sq_a.at[bot_c, :])])),
+    }
+    for role, copies in role_loads.values():
+        @pl.when(role)
+        def _():
+            for cp in copies:
+                cp.start()
+
+    def c_copy(kind):
+        src, rows, where = ((qc0_hbm, top_c, peers[Y_BIT]), (qc1_hbm, bot_c, peers[Z_BIT]))[kind]
+        return remote(src, sq_b.at[rows, :], c_send.at[kind], c_recv.at[kind], where)
+
+    c_sends = (is_late, is_a)
+
+    def spread(terms, groups, tiles):
+        def body(g, _):
+            rows = pl.ds(pl.multiple_of(g * 8, 8), 8)
+            for j in range(tiles):
+                cc = pl.ds(128 * j, 128)
+                val = terms[0][rows, cc]
+                for other in terms[1:]:
+                    val = val + other[rows, cc]
+                s_v[pl.ds(g * (8 * tiles) + j, 8, stride=tiles), :] = val
+            return 0
+
+        lax.fori_loop(0, groups, body, 0)
 
     loads[0].wait()
 
@@ -257,10 +285,19 @@
     for cp in loads[1:]:
         cp.wait()
 
-    @pl.when(jnp.logical_not(is_late))
+    @pl.when(is_late)
     def _():
-        load_s.wait()
-        own_update()
+        c_copy(0).start()
+
+    for name, terms, groups, tiles in (('a', (sq_a, sq_b), 96, 6), ('b', (wide_a, wide_b), 24, 24)):
+        role, copies = role_loads[name]
+
+        @pl.when(role)
+        def _():
+            for cp in copies:
+                cp.wait()
+            spread(terms, groups, tiles)
+            own_update()
 
     for ch in range(N_PRE):
         yz_take(0, ch)
@@ -271,6 +308,10 @@
         x_sum(ch)
         yz_start(0, ch)
         yz_start(1, ch)
+        if ch == N_PRE:
+            @pl.when(is_a)
+            def _():
+                c_copy(1).start()
     for ch in range(N_PRE, N_CH):
         yz_take(0, ch)
         yz_take(1, ch)
@@ -283,13 +324,16 @@
             for kind in (2, 3):
                 yz_take(kind, ch)
 
-        def body(g, _):
-            rows = pl.ds(pl.multiple_of(g * 8, 8), 8)
-            for j in range(24):
-                s_v[pl.ds(g * 192 + j, 8, stride=24), :] = part[rows, 128 * j:128 * (j + 1)]
-            return 0
-
-        lax.fori_loop(0, 24, body, 0)
+        spread((part,), 24, 24)
+        own_update()
+
+    @pl.when(is_c)
+    def _():
+        for cp in role_loads['c'][1]:
+            cp.wait()
+        for kind in (0, 1):
+            c_copy(kind).wait_recv()
+        spread((sq_a, sq_b), 96, 6)
         own_update()
 
     for step in range(3):
@@ -313,36 +357,42 @@
             @pl.when(yz_sends[kind])
             def _():
                 yz_copy(kind, ch).wait_send()
+    for kind in (0, 1):
+        @pl.when(c_sends[kind])
+        def _():
+            c_copy(kind).wait_send()
     for cp in outs:
         cp.wait()
 
 
-def tail(p_d0, g_d1, s_abc, master, adam_m, adam_v):
+def tail(*args):
     any_spec = pl.BlockSpec(memory_space=pl.ANY)
     f32, bf16 = jnp.float32, jnp.bfloat16
     dma = pltpu.SemaphoreType.DMA
-    shard = jax.ShapeDtypeStruct((SHARD_ROWS, 128), f32)
-    state = pltpu.VMEM((SHARD_ROWS, 128), f32)
+    shard = pltpu.VMEM((SHARD_ROWS, 128), f32)
+    half = pltpu.VMEM((96, 3072), f32)
     return pl.pallas_call(
         tail_kernel,
-        out_shape=(shard, shard, shard, jax.ShapeDtypeStruct((16 * SHARD_ROWS, 128), bf16)),
-        in_specs=[any_spec] * 6,
+        out_shape=(shard, shard, shard, pltpu.VMEM((16 * SHARD_ROWS, 128), bf16)),
+        in_specs=[any_spec] * 13,
         out_specs=[any_spec] * 4,
         scratch_shapes=[
             pltpu.VMEM((192, REST_COLS), bf16), pltpu.VMEM((3, 192, REST_COLS), bf16), pltpu.VMEM((192, 3072), f32),
-            pltpu.VMEM((96, 3072), f32), pltpu.VMEM((96, 3072), f32), pltpu.VMEM((96, 3072), f32),
-            pltpu.VMEM((96, 3072), f32), state, state, state, state, pltpu.VMEM((SHARD_ROWS, 128), bf16),
-            dma((6,)), dma((4,)), dma((3, N_CH - N_PRE)), dma((3, N_CH - N_PRE)), dma((4, N_CH)), dma((4, N_CH)),
-            dma((6, 3, 8)), dma((6, 8)), dma((6, 8)), dma((6, 8)),
+            half, half, half, half, pltpu.VMEM((768, 768), f32), pltpu.VMEM((768, 768), f32),
+            pltpu.VMEM((192, 3072), f32), pltpu.VMEM((192, 3072), f32),
+            shard, shard, shard, shard, pltpu.VMEM((SHARD_ROWS, 128), bf16),
+            dma((9,)), dma((4,)), dma((2,)), dma((2,)),
+            dma((3, N_CH - N_PRE)), dma((3, N_CH - N_PRE)), dma((4, N_CH)), dma((4, N_CH)),
+            dma((N_PIECE, 3, 8)), dma((N_PIECE, 8)), dma((N_PIECE, 8)), dma((N_PIECE, 8)),
         ],
-        compiler_params=pltpu.CompilerParams(collective_id=0, has_side_effects=True, vmem_limit_bytes=48 << 20),
+        compiler_params=pltpu.CompilerParams(collective_id=0, has_side_effects=True, vmem_limit_bytes=31 << 20),
         name="tail",
-    )(p_d0, g_d1, s_abc, master, adam_m, adam_v)
+    )(*args)
 
 
 def solution(mesh):
     def inner_step(x_one, dy_one, w1_in, w1_out, w2_in, w2_out, master, adam_m, adam_v):
-        zi, yi, xi = (lax.axis_index(a) for a in AXES)
+        xi = lax.axis_index('dpx')
         f32, bf16 = jnp.float32, jnp.bfloat16
 
         def mm(spec, a, b):
@@ -362,40 +412,27 @@
         x_b = send_x(g_b.reshape(4, 192, 3072), xi)
         p_a = add_x(x_a)
         dz_two, (p_a,) = after(dz_two, p_a)
-        one_a = send_one(p_a, 0, 0)
+        one_a = shift_z(p_a, (0, 1), 0, 0)
         dx_two = (dy_one.astype(f32) + mm('tf,df->td', dz_two, w2_in)).astype(bf16)
         g_c = mm('tf,td->fd', h_one, dx_two).astype(bf16)
         x_c = send_x(g_c.reshape(4, 768, 768), xi)
         p_b = add_x(x_b)
-        q_a = add_one(one_a)
-        dx_two, (p_b, qa0, qa1) = after(dx_two, p_b, *q_a)
-        two_a = send_two((qa0, qa1), 0, 0)
+        dx_two, (p_b, q_a) = after(dx_two, p_b, p_a + one_a)
+        two_a = shift_y(q_a, (0,), 0, 0)
         one_b = send_one(p_b, 0, 1)
-
-        def slope_grad(lo, hi):
-            up = mm('td,fd->tf', dx_two, w1_out[lo:hi])
-            return (up * gelu_slope(z_one[:, lo:hi].astype(f32))).astype(bf16)
-
-        dz_pre = slope_grad(0, PRE_COLS)
-        s_a = add_two(two_a).reshape(-1)
-        q_b = add_one(one_b)
-        dz_pre, (qb0, qb1, s_a) = after(dz_pre, *q_b, s_a)
+        dz_one = (mm('td,fd->tf', dx_two, w1_out) * gelu_slope(z_one.astype(f32))).astype(bf16)
+        p_c = add_x(x_c)
+        dz_one, (qb0, qb1, p_c) = after(dz_one, *add_one(one_b), p_c)
         two_b = send_two((qb0, qb1), 0, 1)
-        g_d0 = mm('td,tf->df', x_one, dz_pre).astype(bf16)
+        one_c = send_one(p_c, 1, 0, C_TOP)
+        g_d0 = mm('td,tf->df', x_one, dz_one[:, :PRE_COLS]).astype(bf16)
         x_d0 = send_x(g_d0.reshape(4, 192, PRE_COLS), xi)
-        p_c = add_x(x_c)
-        dx_two, (p_c,) = after(dx_two, p_c)
-        one_c = send_one(p_c, 1, 0)
-        dz_rest = slope_grad(PRE_COLS, 3072)
-        s_b = add_two(two_b).reshape(-1)
-        q_c = add_one(one_c)
-        dz_rest, (qc0, qc1, s_b) = after(dz_rest, *q_c, s_b)
-        two_c = send_two((qc0, qc1), 1, 0)
-        g_d1 = mm('td,tf->df', x_one, dz_rest).astype(bf16)
-        s_c = add_two(two_c).reshape(-1)
-        s_abc = jnp.where(zi == 0, jnp.where(yi == 0, s_a, s_b), s_c)
+        g_d1 = mm('td,tf->df', x_one, dz_one[:, PRE_COLS:]).astype(bf16)
+        qc0, qc1 = add_one(one_c)
         flat = lambda t: t.reshape(SHARD_ROWS, 128)
-        new_master, new_m, new_v, weights = tail(add_x(x_d0), g_d1, flat(s_abc), flat(master), flat(adam_m), flat(adam_v))
+        new_master, new_m, new_v, weights = tail(
+            add_x(x_d0), g_d1, q_a, two_a, qb0, qb1, two_b[2], two_b[3], qc0, qc1,
+            flat(master), flat(adam_m), flat(adam_v))
         return new_master.reshape(-1), new_m.reshape(-1), new_v.reshape(-1), weights.reshape(-1)
 
     in_specs = (P(AXES, None), P(AXES, None), P(), P(), P(), P(), P(AXES), P(AXES), P(AXES))

time: 580 us -> 556 us (0.959)
  waiting for transfers between devices: 21.7 us -> 67.8 us
  Pallas kernels: 148 us -> 125 us
  local copies, waits for them, and re-layouts: 44.8 us -> 24.2 us
  starting transfers between devices: 46.6 us -> 26.3 us
  other arithmetic: 20.2 us -> 12.2 us
    ppermute x12, waiting for transfers between devices: 21.6 us -> 54.4 us  [send_x(): got.append(lax.ppermute(send, 'dpx', [(i, i ^ k) for i in range(4)]))]
    pallas_call x1, Pallas kernels: 148 us -> 125 us  [tail(): pl.pallas_call(tail_kernel, out_shape=(shard, shard, shard, pltpu.VMEM((1...]
    ppermute x6 -> x4, starting transfers between devices: 21.5 us -> 9.22 us  [shift_z(): return lax.ppermute(val, AXES, pairs)]
    unnamed x41 -> x36, local copies, waits for them, and re-layouts: 29.2 us -> 18 us
    ppermute x6 -> x4, waiting for transfers between devices: 0.02 us -> 7.5 us  [shift_z(): return lax.ppermute(val, AXES, pairs)]
    reshape x2 -> x0, local copies, waits for them, and re-layouts: 6.44 us -> none  [the longest x1 3.22 us: inner_step(): s_a = add_two(two_a).reshape(-1)]
    ppermute x6 -> x4, waiting for transfers between devices: 0.02 us -> 5.9 us  [shift_y(): return lax.ppermute(val, AXES, pairs)]
    ppermute x6 -> x4, starting transfers between devices: 13.5 us -> 8.09 us  [shift_y(): return lax.ppermute(val, AXES, pairs)]
  transfers between devices with their start and end apart: 24 -> 20, of which waited for: 3 -> 5; matrix products, arithmetic and copies ran while one was open for 36% -> 36% of each run, Pallas kernels for 0% -> 0%
where the time goes in v2:
time: 556 us; the launch traced here: 549 us
  matrix products  293 us (53%)
  Pallas kernels  125 us (22%)
  waiting for transfers between devices  67.8 us (12%)
  starting transfers between devices  26.3 us (5%)
  local copies, waits for them, and re-layouts  24.2 us (4%)
  other arithmetic  12.2 us (2%)
    dot_general x11, matrix products, mm(): return jnp.einsum(spec, a, b, preferred_element_type=f32)  293 us
    pallas_call x1, Pallas kernels, tail(): pl.pallas_call(tail_kernel, out_shape=(shard, shard, shard, pltpu.VMEM((1...  125 us
    ppermute x12, waiting for transfers between devices, send_x(): got.append(lax.ppermute(send, 'dpx', [(i, i ^ k) for i in range(4)]))  54.4 us
    unnamed x36, local copies, waits for them, and re-layouts  18 us
  transfers between devices with their start and end apart: 20, of which 5 were waited for; matrix products, arithmetic and copies ran while one was open for 36% of the time, Pallas kernels for 0%

profile of v2, /device:TPU:5, one launch (start us, length us, event | category | flops | bytes accessed | tf_op | source)
XLA Modules:
  0.0 549.5 jit_solution(15126766113718217798)
XLA Ops:
  0.7 30.3 %fusion.1 = (bf16[4096,3072]{1,0:T(8,128)(2,1)}, bf16[4096,3072]{1,0:T(8,128)(2,1)}) fusion(bf16[4096,768]{1,0:T(8,128)(2,1)} %param.9, bf16[768,3072]{1,0:T(8,128)(2,1)} %param.11), kind=kOutput, calls=%fused_computation.13 | convolution fusion | flops 19415433216 | bytes 61341696 | tf_op jit(solution)/shard_map/td,df->tf/dot_general | solution.py:399
  31.0 24.4 %add_convert_fusion.1 = bf16[4096,768]{1,0:T(8,128)(2,1)} fusion(bf16[4096,768]{1,0:T(8,128)(2,1)S(1)} %copy-done.8, bf16[4096,3072]{1,0:T(8,128)(2,1)} %get-tuple-element.21, bf16[3072,768]{1,0:T(8,128)(2,1)S(1)} %copy-done.9), kind=kOutput, calls=%fused_computation.43 | convolution fusion | flops 19336790016 | bytes 42467328 | tf_op jit(solution)/shard_map/tf,fd->td/dot_general | solution.py:399
  55.4 29.3 %fusion.5 = (bf16[4096,3072]{1,0:T(8,128)(2,1)}, bf16[4096,3072]{1,0:T(8,128)(2,1)}) fusion(bf16[4096,768]{1,0:T(8,128)(2,1)} %add_convert_fusion.1, bf16[768,3072]{1,0:T(8,128)(2,1)S(1)} %bitcast.87), kind=kOutput, calls=%fused_computation.17 | convolution fusion | flops 19415433216 | bytes 61341696 | tf_op jit(solution)/shard_map/td,df->tf/dot_general | solution.py:399
  84.8 25.3 %convolution_convert_fusion.4 = bf16[3072,768]{1,0:T(8,128)(2,1)S(1)} fusion(bf16[4096,3072]{1,0:T(8,128)(2,1)} %get-tuple-element.23, bf16[4096,768]{1,0:T(8,128)(2,1)} %param.10), kind=kOutput, calls=%fused_computation.46 | convolution fusion | flops 19329712128 | bytes 36175872 | tf_op jit(solution)/shard_map/tf,td->fd/dot_general | solution.py:399
  116.4 38.2 %fusion.23 = bf16[4096,3072]{1,0:T(8,128)(2,1)} fusion(bf16[4096,3072]{1,0:T(8,128)(2,1)} %get-tuple-element.22, bf16[4096,768]{1,0:T(8,128)(2,1)} %param.10, bf16[3072,768]{1,0:T(8,128)(2,1)} %param.14), kind=kOutput, calls=%fused_computation.35 | convolution fusion | flops 19465764864 | bytes 61341696 | tf_op jit(solution)/shard_map/td,fd->tf/dot_general | solution.py:399
  154.6 23.9 %convolution_convert_fusion.3 = bf16[768,3072]{1,0:T(8,128)(2,1)S(1)} fusion(bf16[4096,768]{1,0:T(8,128)(2,1)S(1)} %bitcast.91, bf16[4096,3072]{1,0:T(8,128)(2,1)} %fusion.23), kind=kOutput, calls=%fused_computation.45 | convolution fusion | flops 19329712128 | bytes 36175872 | tf_op jit(solution)/shard_map/td,tf->df/dot_general | solution.py:399
  178.6 2.3 copy-done.3
  184.9 2.5 fusion.39
  187.4 27.0 %add_convert_fusion = bf16[4096,768]{1,0:T(8,128)(2,1)} fusion(bf16[4096,768]{1,0:T(8,128)(2,1)} %param.10, bf16[4096,3072]{1,0:T(8,128)(2,1)} %fusion.23, bf16[768,3072]{1,0:T(8,128)(2,1)} %param.13), kind=kOutput, calls=%fused_computation.42 | convolution fusion | flops 19336790016 | bytes 42467328 | tf_op jit(solution)/shard_map/tf,df->td/dot_general | solution.py:399
  215.7 25.6 %convolution_convert_fusion.2 = bf16[3072,768]{1,0:T(8,128)(2,1)S(1)} fusion(bf16[4096,3072]{1,0:T(8,128)(2,1)} %get-tuple-element.21, bf16[4096,768]{1,0:T(8,128)(2,1)} %add_convert_fusion), kind=kOutput, calls=%fused_computation.44 | convolution fusion | flops 19329712128 | bytes 36175872 | tf_op jit(solution)/shard_map/tf,td->fd/dot_general | solution.py:399
  245.6 23.5 %collective-permute-done.10 = bf16[768,768]{1,0:T(8,128)(2,1)S(1)} collective-permute-done((bf16[768,768]{1,0:T(8,128)(2,1)S(1)}, bf16[768,768]{1,0:T(8,128)(2,1)S(1)}, u32[]{:S(2)}, u32[]{:S(2)}) %collective-permute-start.10) | collective-permute-done | bytes 1179680 | tf_op jit(solution)/shard_map/ppermute | solution.py:35
  269.1 25.6 %collective-permute-done.11 = bf16[768,768]{1,0:T(8,128)(2,1)S(1)} collective-permute-done((bf16[768,768]{1,0:T(8,128)(2,1)S(1)}, bf16[768,768]{1,0:T(8,128)(2,1)S(1)}, u32[]{:S(2)}, u32[]{:S(2)}) %collective-permute-start.11) | collective-permute-done | bytes 1179680 | tf_op jit(solution)/shard_map/ppermute | solution.py:35
  298.7 37.8 %fusion.22 = bf16[4096,3072]{1,0:T(8,128)(2,1)} fusion(bf16[4096,3072]{1,0:T(8,128)(2,1)} %get-tuple-element.27, bf16[4096,768]{1,0:T(8,128)(2,1)} %add_convert_fusion, bf16[3072,768]{1,0:T(8,128)(2,1)S(1)} %bitcast.89), kind=kOutput, calls=%fused_computation.34 | convolution fusion | flops 19465764864 | bytes 61341696 | tf_op jit(solution)/shard_map/td,fd->tf/dot_general | solution.py:399
  337.7 4.1 collective-permute-start.19
  341.8 15.1 %fusion.28 = bf16[1536,768]{0,1:T(8,128)(2,1)S(1)} fusion(bf16[4096,768]{1,0:T(8,128)(2,1)} %param.9, bf16[4096,3072]{1,0:T(8,128)(2,1)} %fusion.22), kind=kOutput, calls=%fused_computation.47 | convolution fusion | flops 9664856064 | bytes 21233664 | tf_op jit(solution)/shard_map/td,tf->df/dot_general | solution.py:399
  361.7 5.1 collective-permute-start.18
  368.4 5.4 collective-permute-done.13
  375.9 16.1 %fusion.34.gd_hbm = bf16[768,1536]{1,0:T(8,128)(2,1)} fusion(bf16[4096,768]{1,0:T(8,128)(2,1)} %param.9, bf16[4096,3072]{1,0:T(8,128)(2,1)} %fusion.22), kind=kOutput, calls=%fused_computation.49 | convolution fusion | flops 9664856064 | bytes 21233664 | tf_op jit(solution)/shard_map/td,tf->df/dot_general | solution.py:399
  393.0 2.7 fusion.40.p_hbm
  395.7 7.5 %collective-permute-done.18 = f32[576,768]{1,0:T(8,128)} collective-permute-done((f32[576,768]{1,0:T(8,128)S(1)}, f32[576,768]{1,0:T(8,128)}, u32[]{:S(2)}, u32[]{:S(2)}) %collective-permute-start.18) | collective-permute-done | bytes 1769504 | tf_op jit(solution)/shard_map/ppermute | solution.py:46
  403.2 2.9 slice_add_fusion.3.qc0_hbm
  406.1 5.9 %collective-permute-done.15.ra_hbm = f32[768,768]{1,0:T(8,128)S(1)} collective-permute-done((f32[768,768]{1,0:T(8,128)S(1)}, f32[768,768]{1,0:T(8,128)S(1)}, u32[]{:S(2)}, u32[]{:S(2)}) %collective-permute-start.15) | collective-permute-done | bytes 2359328 | tf_op jit(solution)/shard_map/ppermute | solution.py:51
  413.4 124.5 %tail.1 = (f32[4608,128]{1,0:T(8,128)S(1)}, f32[4608,128]{1,0:T(8,128)S(1)}, f32[4608,128]{1,0:T(8,128)S(1)}, bf16[73728,128]{1,0:T(8,128)(2,1)S(1)}) custom-call(f32[192,1536]{1,0:T(8,128)} %fusion.40.p_hbm, bf16[768,1536]{1,0:T(8,128)(2,1)} %fusion.34.gd_hbm, f32[768,768]{1,0:T(8,128)} %copy-done, f32[768,768]{1,0:T(8,128)} %copy-done.5, ...), custom_call_target="tpu_custom_call" | custom-call | tf_op jit(solution)/shard_map/tail/pallas_call | solution.py:374
  537.9 6.7 %copy.22 = bf16[9437184]{0:T(1024)(128)(2,1)} copy(bf16[9437184]{0:T(1024)(128)(2,1)S(1)} %bitcast.71) | data formatting | bytes 37748736
  (82 shorter events, 36.5 us)
Async XLA Ops:
  0.7 54.8 %slice-start = ((s8[4718592]{0:T(1024)(128)(4,1)}), s8[4194304]{0:T(1024)(128)(4,1)S(1)}, s32[]{:S(2)}) async-start(s8[4718592]{0:T(1024)(128)(4,1)} %bitcast.86), calls=%async_computation | async-start | bytes 8388608
  114.1 70.4 %collective-permute-start = (bf16[768,768]{1,0:T(8,128)(2,1)}, bf16[768,768]{1,0:T(8,128)(2,1)S(1)}, u32[]{:S(2)}, u32[]{:S(2)}) collective-permute-start(bf16[768,768]{1,0:T(8,128)(2,1)} %get-tuple-element.44), channel_id=1, source_target_pairs={{0,1},{1,0},{2,3},{3,2},{4,5},{5,4},{6,7},{7,6},{8,9},{9,8},{10,11... | collective-permute-start | bytes 3538952 | tf_op jit(solution)/shard_map/ppermute | solution.py:35
  114.8 70.1 %collective-permute-start.1 = (bf16[768,768]{1,0:T(8,128)(2,1)}, bf16[768,768]{1,0:T(8,128)(2,1)}, u32[]{:S(2)}, u32[]{:S(2)}) collective-permute-start(bf16[768,768]{1,0:T(8,128)(2,1)} %get-tuple-element.46), channel_id=1, source_target_pairs={{0,2},{1,3},{2,0},{3,1},{4,6},{5,7},{6,4},{7,5},{8,10},{9,11},{10,... | collective-permute-start | bytes 3538952 | tf_op jit(solution)/shard_map/ppermute | solution.py:35
  116.0 38.6 %slice-start.4 = ((s8[6291456]{0:T(1024)(128)(4,1)}), s8[4194304]{0:T(1024)(128)(4,1)S(1)}, s32[]{:S(2)}) async-start(s8[6291456]{0:T(1024)(128)(4,1)} %bitcast.90), calls=%async_computation.4 | async-start | bytes 8388608
  116.0 38.6 %slice-start.5 = ((s8[6291456]{0:T(1024)(128)(4,1)}), s8[2097152]{0:T(1024)(128)(4,1)S(1)}, s32[]{:S(2)}) async-start(s8[6291456]{0:T(1024)(128)(4,1)} %bitcast.90), calls=%async_computation.5 | async-start | bytes 4194304
  116.0 68.9 %collective-permute-start.2 = (bf16[768,768]{1,0:T(8,128)(2,1)}, bf16[768,768]{1,0:T(8,128)(2,1)}, u32[]{:S(2)}, u32[]{:S(2)}) collective-permute-start(bf16[768,768]{1,0:T(8,128)(2,1)} %get-tuple-element.45), channel_id=1, source_target_pairs={{0,3},{1,2},{2,1},{3,0},{4,7},{5,6},{6,5},{7,4},{8,11},{9,10},{10,... | collective-permute-start | bytes 3538952 | tf_op jit(solution)/shard_map/ppermute | solution.py:35
  182.8 60.4 %collective-permute-start.3 = (bf16[192,3072]{1,0:T(8,128)(2,1)}, bf16[192,3072]{1,0:T(8,128)(2,1)S(1)}, u32[]{:S(2)}, u32[]{:S(2)}) collective-permute-start(bf16[192,3072]{1,0:T(8,128)(2,1)} %get-tuple-element.41), channel_id=1, source_target_pairs={{0,1},{1,0},{2,3},{3,2},{4,5},{5,4},{6,7},{7,6},{8,9},{9,8},{10,11... | collective-permute-start | bytes 3538952 | tf_op jit(solution)/shard_map/ppermute | solution.py:35
  183.0 60.5 %collective-permute-start.4 = (bf16[192,3072]{1,0:T(8,128)(2,1)}, bf16[192,3072]{1,0:T(8,128)(2,1)S(1)}, u32[]{:S(2)}, u32[]{:S(2)}) collective-permute-start(bf16[192,3072]{1,0:T(8,128)(2,1)} %get-tuple-element.43), channel_id=1, source_target_pairs={{0,2},{1,3},{2,0},{3,1},{4,6},{5,7},{6,4},{7,5},{8,10},{9,11},{10,... | collective-permute-start | bytes 3538952 | tf_op jit(solution)/shard_map/ppermute | solution.py:35
  184.5 59.1 %collective-permute-start.5 = (bf16[192,3072]{1,0:T(8,128)(2,1)}, bf16[192,3072]{1,0:T(8,128)(2,1)S(1)}, u32[]{:S(2)}, u32[]{:S(2)}) collective-permute-start(bf16[192,3072]{1,0:T(8,128)(2,1)} %get-tuple-element.42), channel_id=1, source_target_pairs={{0,3},{1,2},{2,1},{3,0},{4,7},{5,6},{6,5},{7,4},{8,11},{9,10},{10,... | collective-permute-start | bytes 3538952 | tf_op jit(solution)/shard_map/ppermute | solution.py:35
  214.5 80.8 %collective-permute-start.6 = (f32[768,768]{1,0:T(8,128)S(1)}, f32[768,768]{1,0:T(8,128)S(1)}, u32[]{:S(2)}, u32[]{:S(2)}) collective-permute-start(f32[768,768]{1,0:T(8,128)S(1)} %fusion.39), channel_id=1, source_target_pairs={{8,0},{9,1},{10,2},{11,3},{12,4},{13,5},{14,6},{15,7}} | collective-permute-start | bytes 7077896 | tf_op jit(solution)/shard_map/ppermute | solution.py:46
  241.6 27.5 %collective-permute-start.10 = (bf16[768,768]{1,0:T(8,128)(2,1)S(1)}, bf16[768,768]{1,0:T(8,128)(2,1)S(1)}, u32[]{:S(2)}, u32[]{:S(2)}) collective-permute-start(bf16[768,768]{1,0:T(8,128)(2,1)S(1)} %get-tuple-element.40), channel_id=1, source_target_pairs={{0,2},{1,3},{2,0},{3,1},{4,6},{5,7},{6,4},{7,5},{8,10},{9,11},{10,... | collective-permute-start | bytes 3538952 | tf_op jit(solution)/shard_map/ppermute | solution.py:35
  243.2 51.5 %collective-permute-start.11 = (bf16[768,768]{1,0:T(8,128)(2,1)S(1)}, bf16[768,768]{1,0:T(8,128)(2,1)S(1)}, u32[]{:S(2)}, u32[]{:S(2)}) collective-permute-start(bf16[768,768]{1,0:T(8,128)(2,1)S(1)} %get-tuple-element.39), channel_id=1, source_target_pairs={{0,3},{1,2},{2,1},{3,0},{4,7},{5,6},{6,5},{7,4},{8,11},{9,10},{10,... | collective-permute-start | bytes 3538952 | tf_op jit(solution)/shard_map/ppermute | solution.py:35
  243.5 51.2 %collective-permute-start.9 = (bf16[768,768]{1,0:T(8,128)(2,1)S(1)}, bf16[768,768]{1,0:T(8,128)(2,1)S(1)}, u32[]{:S(2)}, u32[]{:S(2)}) collective-permute-start(bf16[768,768]{1,0:T(8,128)(2,1)S(1)} %get-tuple-element.38), channel_id=1, source_target_pairs={{0,1},{1,0},{2,3},{3,2},{4,5},{5,4},{6,7},{7,6},{8,9},{9,8},{10,11... | collective-permute-start | bytes 3538952 | tf_op jit(solution)/shard_map/ppermute | solution.py:35
  295.6 64.6 %copy-start = (f32[768,768]{1,0:T(8,128)}, f32[768,768]{1,0:T(8,128)S(1)}, u32[]{:S(2)}) copy-start(f32[768,768]{1,0:T(8,128)S(1)} %add.118.qa_hbm) | copy-start | bytes 7077892
  295.8 40.7 %collective-permute-start.7 = (f32[96,3072]{1,0:T(8,128)S(1)}, f32[96,3072]{1,0:T(8,128)S(1)}, u32[]{:S(2)}, u32[]{:S(2)}) collective-permute-start(f32[96,3072]{1,0:T(8,128)S(1)} %get-tuple-element.53), channel_id=1, source_target_pairs={{12,4},{13,5},{14,6},{15,7},{8,0},{9,1},{10,2},{11,3}} | collective-permute-start | bytes 3538952 | tf_op jit(solution)/shard_map/ppermute | solution.py:46
  297.4 39.1 %collective-permute-start.8 = (f32[96,3072]{1,0:T(8,128)S(1)}, f32[96,3072]{1,0:T(8,128)S(1)}, u32[]{:S(2)}, u32[]{:S(2)}) collective-permute-start(f32[96,3072]{1,0:T(8,128)S(1)} %get-tuple-element.52), channel_id=1, source_target_pairs={{0,4},{1,5},{2,6},{3,7},{8,12},{9,13},{10,14},{11,15}} | collective-permute-start | bytes 3538952 | tf_op jit(solution)/shard_map/ppermute | solution.py:51
  337.7 29.1 %collective-permute-start.19 = (f32[192,768]{1,0:T(8,128)}, f32[192,768]{1,0:T(8,128)S(1)}, u32[]{:S(2)}, u32[]{:S(2)}) collective-permute-start(f32[192,768]{1,0:T(8,128)} %slice.23), channel_id=1, source_target_pairs={{12,8},{13,9},{14,10},{15,11},{4,0},{5,1},{6,2},{7,3}} | collective-permute-start | bytes 1769480 | tf_op jit(solution)/shard_map/ppermute | solution.py:51
  357.8 9.3 %collective-permute-start.12 = (bf16[192,1536]{1,0:T(8,128)(2,1)S(1)}, bf16[192,1536]{1,0:T(8,128)(2,1)S(1)}, u32[]{:S(2)}, u32[]{:S(2)}) collective-permute-start(bf16[192,1536]{1,0:T(8,128)(2,1)S(1)} %get-tuple-element.47), channel_id=1, source_target_pairs={{0,1},{1,0},{2,3},{3,2},{4,5},{5,4},{6,7},{7,6},{8,9},{9,8},{10,11... | collective-permute-start | bytes 1769480 | tf_op jit(solution)/shard_map/ppermute | solution.py:35
  358.5 15.3 %collective-permute-start.13 = (bf16[192,1536]{1,0:T(8,128)(2,1)S(1)}, bf16[192,1536]{1,0:T(8,128)(2,1)S(1)}, u32[]{:S(2)}, u32[]{:S(2)}) collective-permute-start(bf16[192,1536]{1,0:T(8,128)(2,1)S(1)} %get-tuple-element.49), channel_id=1, source_target_pairs={{0,2},{1,3},{2,0},{3,1},{4,6},{5,7},{6,4},{7,5},{8,10},{9,11},{10,... | collective-permute-start | bytes 1769480 | tf_op jit(solution)/shard_map/ppermute | solution.py:35
  360.1 51.9 %collective-permute-start.15 = (f32[768,768]{1,0:T(8,128)S(1)}, f32[768,768]{1,0:T(8,128)S(1)}, u32[]{:S(2)}, u32[]{:S(2)}) collective-permute-start(f32[768,768]{1,0:T(8,128)S(1)} %add.118.qa_hbm), channel_id=1, source_target_pairs={{4,0},{5,1},{6,2},{7,3}} | collective-permute-start | bytes 7077896 | tf_op jit(solution)/shard_map/ppermute | solution.py:51
  361.7 41.5 %collective-permute-start.18 = (f32[576,768]{1,0:T(8,128)S(1)}, f32[576,768]{1,0:T(8,128)}, u32[]{:S(2)}, u32[]{:S(2)}) collective-permute-start(f32[576,768]{1,0:T(8,128)S(1)} %slice.22), channel_id=1, source_target_pairs={{0,8},{1,9},{2,10},{3,11},{4,12},{5,13},{6,14},{7,15}} | collective-permute-start | bytes 5308424 | tf_op jit(solution)/shard_map/ppermute | solution.py:46
  366.8 26.2 %collective-permute-start.14 = (bf16[192,1536]{1,0:T(8,128)(2,1)}, bf16[192,1536]{1,0:T(8,128)(2,1)}, u32[]{:S(2)}, u32[]{:S(2)}) collective-permute-start(bf16[192,1536]{1,0:T(8,128)(2,1)} %get-tuple-element.48), channel_id=1, source_target_pairs={{0,3},{1,2},{2,1},{3,0},{4,7},{5,6},{6,5},{7,4},{8,11},{9,10},{10,... | collective-permute-start | bytes 1769480 | tf_op jit(solution)/shard_map/ppermute | solution.py:35
  367.1 39.0 %collective-permute-start.16 = (f32[96,3072]{1,0:T(8,128)S(1)}, f32[96,3072]{1,0:T(8,128)}, u32[]{:S(2)}, u32[]{:S(2)}) collective-permute-start(f32[96,3072]{1,0:T(8,128)S(1)} %get-tuple-element.31.qb0_hbm), channel_id=1, source_target_pairs={{0,4},{1,5},{2,6},{3,7}} | collective-permute-start | bytes 3538952 | tf_op jit(solution)/shard_map/ppermute | solution.py:51
  374.6 31.5 %collective-permute-start.17 = (f32[96,3072]{1,0:T(8,128)S(1)}, f32[96,3072]{1,0:T(8,128)}, u32[]{:S(2)}, u32[]{:S(2)}) collective-permute-start(f32[96,3072]{1,0:T(8,128)S(1)} %get-tuple-element.32.qb1_hbm), channel_id=1, source_target_pairs={{12,4},{13,5},{14,6},{15,7}} | collective-permute-start | bytes 3538952 | tf_op jit(solution)/shard_map/ppermute | solution.py:46
  (12 other events, 173.2 us)

commit v3 on v2

--- a/solution.py
+++ b/solution.py
@@ -28,17 +28,17 @@
 
 
 def send_x(blocks, x_idx):
-    own = lax.dynamic_index_in_dim(blocks, x_idx, 0, keepdims=False)
-    got = [own]
+    got = []
     for k in (2, 3, 1):
         send = lax.dynamic_index_in_dim(blocks, x_idx ^ k, 0, keepdims=False)
         got.append(lax.ppermute(send, 'dpx', [(i, i ^ k) for i in range(4)]))
     return got
 
 
-def add_x(got):
-    total = got[3].astype(jnp.float32) + got[0].astype(jnp.float32)
-    return total + (got[1].astype(jnp.float32) + got[2].astype(jnp.float32))
+def add_x(blocks, x_idx, got):
+    own = lax.dynamic_index_in_dim(blocks, x_idx, 0, keepdims=False)
+    total = got[2].astype(jnp.float32) + own.astype(jnp.float32)
+    return total + (got[0].astype(jnp.float32) + got[1].astype(jnp.float32))
 
 
 def shift_z(val, y_rel, zo, yo):
@@ -75,18 +75,18 @@
 PIECE_ROWS = SHARD_ROWS // N_PIECE
 CH_COLS = 512
 N_CH = 6
-N_PRE = 3
-PRE_COLS = N_PRE * CH_COLS
-REST_COLS = 3072 - PRE_COLS
+N_PRE = 4
+PIECE_COLS = 1024
 X_BIT, Y_BIT, Z_BIT = 1, 2, 4
 ADAM_ROWS = 96
-C_TOP = 576
+C_TOP = 480
 ORDERS = ((X_BIT, Y_BIT, Z_BIT), (Y_BIT, Z_BIT, X_BIT), (Z_BIT, X_BIT, Y_BIT)) * 2
 
 
-def tail_kernel(p_hbm, gd_hbm, qa_hbm, ra_hbm, qb0_hbm, qb1_hbm, rb0_hbm, rb1_hbm, qc0_hbm, qc1_hbm,
+def tail_kernel(gd0_hbm, gd1_hbm, gd_hbm, d0k2, d0k3, d0k1, d1k2, d1k3, d1k1,
+                qa_hbm, ra_hbm, qb0_hbm, qb1_hbm, rb0_hbm, rb1_hbm, pc0_hbm, pc1_hbm, rc0_hbm, rc1_hbm,
                 mst_hbm, m_hbm, v_hbm, omst_hbm, om_hbm, ov_hbm, w_hbm,
-                own, xrecv, part, a1, b1, a2, b2, sq_a, sq_b, wide_a, wide_b, s_v, mst_v, m_v, v_v, w_v,
+                own, xrecv, part, a1, b1, a2, b2, sq_a, sq_b, c_a, c_b, wide_a, wide_b, s_v, mst_v, m_v, v_v, w_v,
                 ld_sem, st_sem, c_send, c_recv, xs_send, xs_recv, yz_send, yz_recv, ag_send, ag_recv, dd_send, dd_recv):
     z, y, x = (lax.axis_index(a) for a in AXES)
     ny, nz = 1 - y, 1 - z
@@ -110,35 +110,45 @@
         return pltpu.make_async_remote_copy(src_ref=src, dst_ref=dst, send_sem=send, recv_sem=recv,
                                             device_id=where, device_id_type=pl.DeviceIdType.MESH)
 
+    def cols(ch):
+        return pl.ds(ch * CH_COLS, CH_COLS)
+
     def xs_copy(k, ch):
         lo = (ch - N_PRE) * CH_COLS
         to = x_peer(k)
         return remote(gd_hbm.at[pl.ds(to * 192, 192), pl.ds(lo, CH_COLS)],
-                      xrecv.at[k - 1, :, pl.ds(lo, CH_COLS)],
+                      xrecv.at[k - 1, :, cols(ch)],
                       xs_send.at[k - 1, ch - N_PRE], xs_recv.at[k - 1, ch - N_PRE], {'dpx': to})
 
     for ch in range(N_PRE, N_CH):
         for k in (2, 3, 1):
             xs_copy(k, ch).start()
 
-    loads = [pltpu.make_async_copy(p_hbm, part.at[:, pl.ds(0, PRE_COLS)], ld_sem.at[0]),
-             pltpu.make_async_copy(gd_hbm.at[pl.ds(x * 192, 192), :], own, ld_sem.at[1]),
-             pltpu.make_async_copy(mst_hbm, mst_v, ld_sem.at[2]),
-             pltpu.make_async_copy(m_hbm, m_v, ld_sem.at[3]),
-             pltpu.make_async_copy(v_hbm, v_v, ld_sem.at[4])]
+    mine = pl.ds(x * 192, 192)
+    pre = []
+    for part_no, (grad, got) in enumerate(((gd0_hbm, (d0k1, d0k2, d0k3)), (gd1_hbm, (d1k1, d1k2, d1k3)))):
+        cc = pl.ds(part_no * PIECE_COLS, PIECE_COLS)
+        pre.append((grad.at[mine, :], own.at[:, cc]))
+        pre.extend((got[k], xrecv.at[k, :, cc]) for k in range(3))
+    state = [(gd_hbm.at[mine, :], own.at[:, pl.ds(2 * PIECE_COLS, PIECE_COLS)]),
+             (mst_hbm, mst_v), (m_hbm, m_v), (v_hbm, v_v)]
+    loads = [pltpu.make_async_copy(src, dst, ld_sem.at[i]) for i, (src, dst) in enumerate(pre + state)]
     for cp in loads:
         cp.start()
     is_a, is_b, is_c = (z == 0) & (y == 0), (z == 0) & (y == 1), (z == 1) & (y == 0)
 
-    def fetch(items):
-        return [pltpu.make_async_copy(src, dst, ld_sem.at[5 + i]) for i, (src, dst) in enumerate(items)]
+    def fetch(items, base=12):
+        return [pltpu.make_async_copy(src, dst, ld_sem.at[base + i]) for i, (src, dst) in enumerate(items)]
 
     top_c, bot_c = pl.ds(0, C_TOP), pl.ds(C_TOP, 768 - C_TOP)
     role_loads = {
         'a': (is_a, fetch([(qa_hbm, sq_a), (ra_hbm, sq_b)])),
         'b': (is_b, fetch([(qb0_hbm, wide_a.at[pl.ds(0, 96), :]), (qb1_hbm, wide_a.at[pl.ds(96, 96), :]),
                            (rb0_hbm, wide_b.at[pl.ds(0, 96), :]), (rb1_hbm, wide_b.at[pl.ds(96, 96), :])])),
-        'c': (is_c, fetch([(qc0_hbm, sq_a.at[top_c, :]), (qc1_hbm, sq_a.at[bot_c, :])])),
+        'c': (is_c, fetch([(pc0_hbm, c_a.at[top_c, :]), (pc1_hbm, c_a.at[bot_c, :]),
+                           (rc0_hbm, c_b.at[top_c, :]), (rc1_hbm, c_b.at[bot_c, :])])),
+        'send0': (is_late, fetch([(pc0_hbm, c_a.at[top_c, :]), (rc0_hbm, c_b.at[top_c, :])], 16)),
+        'send1': (is_a, fetch([(pc1_hbm, c_a.at[bot_c, :]), (rc1_hbm, c_b.at[bot_c, :])], 16)),
     }
     for role, copies in role_loads.values():
         @pl.when(role)
@@ -147,10 +157,22 @@
                 cp.start()
 
     def c_copy(kind):
-        src, rows, where = ((qc0_hbm, top_c, peers[Y_BIT]), (qc1_hbm, bot_c, peers[Z_BIT]))[kind]
-        return remote(src, sq_b.at[rows, :], c_send.at[kind], c_recv.at[kind], where)
+        rows, where = ((top_c, peers[Y_BIT]), (bot_c, peers[Z_BIT]))[kind]
+        return remote(c_a.at[rows, :], sq_b.at[rows, :], c_send.at[kind], c_recv.at[kind], where)
 
     c_sends = (is_late, is_a)
+
+    def c_add(kind):
+        for cp in role_loads['send%d' % kind][1]:
+            cp.wait()
+        lo, count = ((0, C_TOP), (C_TOP, 768 - C_TOP))[kind]
+
+        def body(i, _):
+            rows = pl.ds(pl.multiple_of(lo + i * 16, 16), 16)
+            c_a[rows, :] += c_b[rows, :]
+            return 0
+
+        lax.fori_loop(0, count // 16, body, 0)
 
     def spread(terms, groups, tiles):
         def body(g, _):
@@ -165,10 +187,8 @@
 
         lax.fori_loop(0, groups, body, 0)
 
-    loads[0].wait()
-
-    def cols(ch):
-        return pl.ds(ch * CH_COLS, CH_COLS)
+    for cp in loads[:len(pre)]:
+        cp.wait()
 
     top, bot = pl.ds(0, 96), pl.ds(96, 96)
 
@@ -201,15 +221,14 @@
             lax.fori_loop(0, 12, body, 0)
 
     def x_sum(ch):
-        lo = (ch - N_PRE) * CH_COLS
-        for k in (2, 3, 1):
-            xs_copy(k, ch).wait_recv()
+        if ch >= N_PRE:
+            for k in (2, 3, 1):
+                xs_copy(k, ch).wait_recv()
 
         def body(i, _):
             rows = pl.ds(pl.multiple_of(i * 16, 16), 16)
-            cc = pl.ds(lo, CH_COLS)
-            part[rows, cols(ch)] = ((own[rows, cc].astype(f32) + xrecv[0, rows, cc].astype(f32))
-                                    + (xrecv[1, rows, cc].astype(f32) + xrecv[2, rows, cc].astype(f32)))
+            part[rows, cols(ch)] = ((own[rows, cols(ch)].astype(f32) + xrecv[0, rows, cols(ch)].astype(f32))
+                                    + (xrecv[1, rows, cols(ch)].astype(f32) + xrecv[2, rows, cols(ch)].astype(f32)))
             return 0
 
         lax.fori_loop(0, 12, body, 0)
@@ -280,14 +299,20 @@
         put.wait()
 
     for ch in range(N_PRE):
+        x_sum(ch)
         yz_start(0, ch)
         yz_start(1, ch)
-    for cp in loads[1:]:
+    for cp in loads[len(pre):]:
         cp.wait()
 
     @pl.when(is_late)
     def _():
+        c_add(0)
         c_copy(0).start()
+
+    @pl.when(is_a)
+    def _():
+        c_add(1)
 
     for name, terms, groups, tiles in (('a', (sq_a, sq_b), 96, 6), ('b', (wide_a, wide_b), 24, 24)):
         role, copies = role_loads[name]
@@ -333,7 +358,7 @@
             cp.wait()
         for kind in (0, 1):
             c_copy(kind).wait_recv()
-        spread((sq_a, sq_b), 96, 6)
+        spread((c_a, c_b, sq_b), 96, 6)
         own_update()
 
     for step in range(3):
@@ -371,23 +396,51 @@
     dma = pltpu.SemaphoreType.DMA
     shard = pltpu.VMEM((SHARD_ROWS, 128), f32)
     half = pltpu.VMEM((96, 3072), f32)
+    square = pltpu.VMEM((768, 768), f32)
     return pl.pallas_call(
         tail_kernel,
         out_shape=(shard, shard, shard, pltpu.VMEM((16 * SHARD_ROWS, 128), bf16)),
-        in_specs=[any_spec] * 13,
+        in_specs=[any_spec] * len(args),
         out_specs=[any_spec] * 4,
         scratch_shapes=[
-            pltpu.VMEM((192, REST_COLS), bf16), pltpu.VMEM((3, 192, REST_COLS), bf16), pltpu.VMEM((192, 3072), f32),
-            half, half, half, half, pltpu.VMEM((768, 768), f32), pltpu.VMEM((768, 768), f32),
+            pltpu.VMEM((192, 3072), bf16), pltpu.VMEM((3, 192, 3072), bf16), pltpu.VMEM((192, 3072), f32),
+            half, half, half, half, square, square, square, square,
             pltpu.VMEM((192, 3072), f32), pltpu.VMEM((192, 3072), f32),
             shard, shard, shard, shard, pltpu.VMEM((SHARD_ROWS, 128), bf16),
-            dma((9,)), dma((4,)), dma((2,)), dma((2,)),
+            dma((18,)), dma((4,)), dma((2,)), dma((2,)),
             dma((3, N_CH - N_PRE)), dma((3, N_CH - N_PRE)), dma((4, N_CH)), dma((4, N_CH)),
             dma((N_PIECE, 3, 8)), dma((N_PIECE, 8)), dma((N_PIECE, 8)), dma((N_PIECE, 8)),
         ],
-        compiler_params=pltpu.CompilerParams(collective_id=0, has_side_effects=True, vmem_limit_bytes=31 << 20),
+        compiler_params=pltpu.CompilerParams(collective_id=0, has_side_effects=True, vmem_limit_bytes=38 << 20),
         name="tail",
     )(*args)
+
+
+def slope_product(grad, weight, pre):
+    rows, cols, sub = 1024, 1536, 256
+
+    def kernel(grad_ref, weight_ref, pre_ref, out_ref):
+        for i in range(rows // sub):
+            part = pl.ds(i * sub, sub)
+            up = lax.dot_general(grad_ref[part, :], weight_ref[...], (((1,), (1,)), ((), ())),
+                                 preferred_element_type=jnp.float32)
+            out_ref[part, :] = (up * gelu_slope(pre_ref[part, :].astype(jnp.float32))).astype(jnp.bfloat16)
+
+    tokens, width = grad.shape
+    full = weight.shape[0]
+    return pl.pallas_call(
+        kernel,
+        grid=(full // cols, tokens // rows),
+        in_specs=[pl.BlockSpec((rows, width), lambda j, i: (i, 0)),
+                  pl.BlockSpec((cols, width), lambda j, i: (j, 0)),
+                  pl.BlockSpec((rows, cols), lambda j, i: (i, j))],
+        out_specs=pl.BlockSpec((rows, cols), lambda j, i: (i, j)),
+        out_shape=jax.ShapeDtypeStruct((tokens, full), jnp.bfloat16),
+        compiler_params=pltpu.CompilerParams(vmem_limit_bytes=40 << 20),
+        cost_estimate=pl.CostEstimate(flops=2 * tokens * width * full, bytes_accessed=4 * tokens * full,
+                                      transcendentals=tokens * full),
+        name="slope_product",
+    )(grad, weight, pre)
 
 
 def solution(mesh):
@@ -407,31 +460,37 @@
         z_two, h_two = lax.optimization_barrier((z_two, h_two))
         g_a = mm('tf,td->fd', h_two, dy_one).astype(bf16)
         x_a = send_x(g_a.reshape(4, 768, 768), xi)
-        dz_two = (mm('td,fd->tf', dy_one, w2_out) * gelu_slope(z_two.astype(f32))).astype(bf16)
+        dz_two = slope_product(dy_one, w2_out, z_two)
         g_b = mm('td,tf->df', x_two, dz_two).astype(bf16)
         x_b = send_x(g_b.reshape(4, 192, 3072), xi)
-        p_a = add_x(x_a)
+        p_a = add_x(g_a.reshape(4, 768, 768), xi, x_a)
         dz_two, (p_a,) = after(dz_two, p_a)
         one_a = shift_z(p_a, (0, 1), 0, 0)
         dx_two = (dy_one.astype(f32) + mm('tf,df->td', dz_two, w2_in)).astype(bf16)
         g_c = mm('tf,td->fd', h_one, dx_two).astype(bf16)
         x_c = send_x(g_c.reshape(4, 768, 768), xi)
-        p_b = add_x(x_b)
+        p_b = add_x(g_b.reshape(4, 192, 3072), xi, x_b)
         dx_two, (p_b, q_a) = after(dx_two, p_b, p_a + one_a)
         two_a = shift_y(q_a, (0,), 0, 0)
         one_b = send_one(p_b, 0, 1)
-        dz_one = (mm('td,fd->tf', dx_two, w1_out) * gelu_slope(z_one.astype(f32))).astype(bf16)
-        p_c = add_x(x_c)
-        dz_one, (qb0, qb1, p_c) = after(dz_one, *add_one(one_b), p_c)
+        dz_one = slope_product(dx_two, w1_out, z_one)
+        dz_one, (qb0, qb1) = after(dz_one, *add_one(one_b))
         two_b = send_two((qb0, qb1), 0, 1)
+
+        def last_piece(grad, i):
+            return mm('td,tf->df', x_one, grad[:, i * PIECE_COLS:(i + 1) * PIECE_COLS]).astype(bf16)
+
+        g_d0 = last_piece(dz_one, 0)
+        x_d0 = send_x(g_d0.reshape(4, 192, PIECE_COLS), xi)
+        p_c = add_x(g_c.reshape(4, 768, 768), xi, x_c)
+        dz_one, (p_c,) = after(dz_one, p_c)
         one_c = send_one(p_c, 1, 0, C_TOP)
-        g_d0 = mm('td,tf->df', x_one, dz_one[:, :PRE_COLS]).astype(bf16)
-        x_d0 = send_x(g_d0.reshape(4, 192, PRE_COLS), xi)
-        g_d1 = mm('td,tf->df', x_one, dz_one[:, PRE_COLS:]).astype(bf16)
-        qc0, qc1 = add_one(one_c)
+        g_d1 = last_piece(dz_one, 1)
+        x_d1 = send_x(g_d1.reshape(4, 192, PIECE_COLS), xi)
+        g_d2 = last_piece(dz_one, 2)
         flat = lambda t: t.reshape(SHARD_ROWS, 128)
         new_master, new_m, new_v, weights = tail(
-            add_x(x_d0), g_d1, q_a, two_a, qb0, qb1, two_b[2], two_b[3], qc0, qc1,
+            g_d0, g_d1, g_d2, *x_d0, *x_d1, q_a, two_a, qb0, qb1, two_b[2], two_b[3], *one_c,
             flat(master), flat(adam_m), flat(adam_v))
         return new_master.reshape(-1), new_m.reshape(-1), new_v.reshape(-1), weights.reshape(-1)
 

time: 556 us -> 556 us (level)
  matrix products: 293 us -> 218 us
  Pallas kernels: 125 us -> 188 us
  waiting for transfers between devices: 67.8 us -> 80.1 us
    dot_general x11 -> x10, matrix products: 293 us -> 218 us  [mm(): return jnp.einsum(spec, a, b, preferred_element_type=f32)]
    pallas_call x0 -> x2, Pallas kernels: none -> 62.9 us  [slope_product(): pl.pallas_call(kernel, grid=(full // cols, tokens // rows), in_specs=[pl....]
    ppermute x12 -> x15, waiting for transfers between devices: 54.4 us -> 64.5 us  [send_x(): got.append(lax.ppermute(send, 'dpx', [(i, i ^ k) for i in range(4)]))]
    ppermute x4, waiting for transfers between devices: 5.9 us -> 14.5 us  [shift_y(): return lax.ppermute(val, AXES, pairs)]
    ppermute x4, waiting for transfers between devices: 7.5 us -> 1.07 us  [shift_z(): return lax.ppermute(val, AXES, pairs)]
    unnamed x36 -> x60, local copies, waits for them, and re-layouts: 18 us -> 21.7 us
    ppermute x12 -> x15, starting transfers between devices: 9.02 us -> 11.9 us  [send_x(): got.append(lax.ppermute(send, 'dpx', [(i, i ^ k) for i in range(4)]))]
  transfers between devices with their start and end apart: 20 -> 23, of which waited for: 5 -> 7; matrix products, arithmetic and copies ran while one was open for 36% -> 21% of each run, Pallas kernels for 0% -> 11%
where the time goes in v3:
time: 556 us; the launch traced here: 549 us
  matrix products  218 us (39%)
  Pallas kernels  188 us (34%)
  waiting for transfers between devices  80.1 us (14%)
  local copies, waits for them, and re-layouts  27.3 us (5%)
  starting transfers between devices  26.5 us (5%)
  other arithmetic  7.63 us (1%)
    dot_general x10, matrix products, mm(): return jnp.einsum(spec, a, b, preferred_element_type=f32)  218 us
    pallas_call x1, Pallas kernels, tail(): pl.pallas_call(tail_kernel, out_shape=(shard, shard, shard, pltpu.VMEM((1...  125 us
    ppermute x15, waiting for transfers between devices, send_x(): got.append(lax.ppermute(send, 'dpx', [(i, i ^ k) for i in range(4)]))  64.5 us
    pallas_call x2, Pallas kernels, slope_product(): pl.pallas_call(kernel, grid=(full // cols, tokens // rows), in_specs=[pl....  62.9 us
    unnamed x60, local copies, waits for them, and re-layouts  21.7 us
    ppermute x4, waiting for transfers between devices, shift_y(): return lax.ppermute(val, AXES, pairs)  14.5 us
    ppermute x15, starting transfers between devices, send_x(): got.append(lax.ppermute(send, 'dpx', [(i, i ^ k) for i in range(4)]))  11.9 us
  transfers between devices with their start and end apart: 23, of which 7 were waited for; matrix products, arithmetic and copies ran while one was open for 21% of the time, Pallas kernels for 11%

profile of v3, /device:TPU:5, one launch (start us, length us, event | category | flops | bytes accessed | tf_op | source)
XLA Modules:
  0.0 549.3 jit_solution(11309891190687547191)
XLA Ops:
  0.7 30.3 %fusion.1 = (bf16[4096,3072]{1,0:T(8,128)(2,1)}, bf16[4096,3072]{1,0:T(8,128)(2,1)}) fusion(bf16[4096,768]{1,0:T(8,128)(2,1)} %param.9, bf16[768,3072]{1,0:T(8,128)(2,1)} %param.11), kind=kOutput, calls=%fused_computation.5 | convolution fusion | flops 19415433216 | bytes 61341696 | tf_op jit(solution)/shard_map/td,df->tf/dot_general | solution.py:452
  31.0 24.4 %add_convert_fusion.1 = bf16[4096,768]{1,0:T(8,128)(2,1)} fusion(bf16[4096,768]{1,0:T(8,128)(2,1)S(1)} %copy-done.22, bf16[4096,3072]{1,0:T(8,128)(2,1)} %get-tuple-element.22, bf16[3072,768]{1,0:T(8,128)(2,1)S(1)} %copy-done.2), kind=kOutput, calls=%fused_computation.15 | convolution fusion | flops 19336790016 | bytes 42467328 | tf_op jit(solution)/shard_map/tf,fd->td/dot_general | solution.py:452
  55.5 29.3 %fusion.5 = (bf16[4096,3072]{1,0:T(8,128)(2,1)}, bf16[4096,3072]{1,0:T(8,128)(2,1)}) fusion(bf16[4096,768]{1,0:T(8,128)(2,1)} %add_convert_fusion.1, bf16[768,3072]{1,0:T(8,128)(2,1)S(1)} %bitcast.94), kind=kOutput, calls=%fused_computation.9 | convolution fusion | flops 19415433216 | bytes 61341696 | tf_op jit(solution)/shard_map/td,df->tf/dot_general | solution.py:452
  84.8 26.0 %convolution_convert_fusion.4 = bf16[3072,768]{1,0:T(8,128)(2,1)S(1)} fusion(bf16[4096,3072]{1,0:T(8,128)(2,1)} %get-tuple-element.24, bf16[4096,768]{1,0:T(8,128)(2,1)} %grad_ref.1), kind=kOutput, calls=%fused_computation.24 | convolution fusion | flops 19329712128 | bytes 36175872 | tf_op jit(solution)/shard_map/tf,td->fd/dot_general | solution.py:452
  115.8 2.8 copy-done
  118.6 2.3 copy-done.1
  120.9 31.2 %slope_product.2 = bf16[4096,3072]{1,0:T(8,128)(2,1)} custom-call(bf16[4096,768]{1,0:T(8,128)(2,1)S(1)} %copy-done, bf16[3072,768]{1,0:T(8,128)(2,1)S(1)} %copy-done.1, bf16[4096,3072]{1,0:T(8,128)(2,1)} %get-tuple-element.23.pre_ref), custom_call_target="tpu_custom_call" | custom-call | flops 19327352832 | bytes 50331648 | tf_op jit(solution)/shard_map/slope_product/pallas_call | solution.py:431
  152.2 23.8 %convolution_convert_fusion.3 = bf16[768,3072]{1,0:T(8,128)(2,1)S(1)} fusion(bf16[4096,768]{1,0:T(8,128)(2,1)S(1)} %copy-done.23, bf16[4096,3072]{1,0:T(8,128)(2,1)} %slope_product.2), kind=kOutput, calls=%fused_computation.23 | convolution fusion | flops 19329712128 | bytes 36175872 | tf_op jit(solution)/shard_map/td,tf->df/dot_general | solution.py:452
  184.4 24.9 %add_convert_fusion.grad_ref = bf16[4096,768]{1,0:T(8,128)(2,1)S(1)} fusion(bf16[4096,768]{1,0:T(8,128)(2,1)} %grad_ref.1, bf16[4096,3072]{1,0:T(8,128)(2,1)} %slope_product.2, bf16[768,3072]{1,0:T(8,128)(2,1)} %param.13), kind=kOutput, calls=%fused_computation.14 | convolution fusion | flops 19336790016 | bytes 42467328 | tf_op jit(solution)/shard_map/tf,df->td/dot_general | solution.py:452
  210.6 24.2 %convolution_convert_fusion.2 = bf16[3072,768]{1,0:T(8,128)(2,1)S(1)} fusion(bf16[4096,3072]{1,0:T(8,128)(2,1)} %get-tuple-element.22, bf16[4096,768]{1,0:T(8,128)(2,1)S(1)} %add_convert_fusion.grad_ref), kind=kOutput, calls=%fused_computation.22 | convolution fusion | flops 19329712128 | bytes 36175872 | tf_op jit(solution)/shard_map/tf,td->fd/dot_general | solution.py:452
  236.9 3.1 fusion.15
  240.0 22.9 %collective-permute-done.10 = bf16[768,768]{1,0:T(8,128)(2,1)S(1)} collective-permute-done((bf16[768,768]{1,0:T(8,128)(2,1)S(1)}, bf16[768,768]{1,0:T(8,128)(2,1)S(1)}, u32[]{:S(2)}, u32[]{:S(2)}) %collective-permute-start.10) | collective-permute-done | bytes 1179680 | tf_op jit(solution)/shard_map/ppermute | solution.py:34
  262.9 25.3 %collective-permute-done.11 = bf16[768,768]{1,0:T(8,128)(2,1)S(1)} collective-permute-done((bf16[768,768]{1,0:T(8,128)(2,1)S(1)}, bf16[768,768]{1,0:T(8,128)(2,1)S(1)}, u32[]{:S(2)}, u32[]{:S(2)}) %collective-permute-start.11) | collective-permute-done | bytes 1179680 | tf_op jit(solution)/shard_map/ppermute | solution.py:34
  293.0 5.2 collective-permute-start.18
  298.2 31.7 %slope_product.3 = bf16[4096,3072]{1,0:T(8,128)(2,1)} custom-call(bf16[4096,768]{1,0:T(8,128)(2,1)S(1)} %add_convert_fusion.grad_ref, bf16[3072,768]{1,0:T(8,128)(2,1)S(1)} %bitcast.79, bf16[4096,3072]{1,0:T(8,128)(2,1)} %get-tuple-element.28.pre_ref), custom_call_target="tpu_custom_call" | custom-call | flops 19327352832 | bytes 50331648 | tf_op jit(solution)/shard_map/slope_product/pallas_call | solution.py:431
  331.5 11.8 %fusion.20 = bf16[1024,768]{0,1:T(8,128)(2,1)S(1)} fusion(bf16[4096,768]{1,0:T(8,128)(2,1)} %param.9, bf16[4096,3072]{1,0:T(8,128)(2,1)} %slope_product.3), kind=kOutput, calls=%fused_computation.32 | convolution fusion | flops 6443237376 | bytes 16252928 | tf_op jit(solution)/shard_map/td,tf->df/dot_general | solution.py:452
  346.1 11.0 %fusion.17 = bf16[1024,768]{0,1:T(8,128)(2,1)S(1)} fusion(bf16[4096,768]{1,0:T(8,128)(2,1)} %param.9, bf16[4096,3072]{1,0:T(8,128)(2,1)} %slope_product.3), kind=kOutput, calls=%fused_computation.31 | convolution fusion | flops 6443237376 | bytes 16252928 | tf_op jit(solution)/shard_map/td,tf->df/dot_general | solution.py:452
  359.5 4.7 collective-permute-done.16.d1k3
  366.5 3.7 collective-permute-done.12.d0k2
  371.7 8.0 %collective-permute-done.13.d0k3 = bf16[192,1024]{1,0:T(8,128)(2,1)S(1)} collective-permute-done((bf16[192,1024]{1,0:T(8,128)(2,1)S(1)}, bf16[192,1024]{1,0:T(8,128)(2,1)S(1)}, u32[]{:S(2)}, u32[]{:S(2)}) %collective-permute-start.13) | collective-permute-done | bytes 393248 | tf_op jit(solution)/shard_map/ppermute | solution.py:34
  382.3 12.5 %fusion.26.gd_hbm = bf16[768,1024]{1,0:T(8,128)(2,1)} fusion(bf16[4096,768]{1,0:T(8,128)(2,1)} %param.9, bf16[4096,3072]{1,0:T(8,128)(2,1)} %slope_product.3), kind=kOutput, calls=%fused_computation.34 | convolution fusion | flops 6443237376 | bytes 16252928 | tf_op jit(solution)/shard_map/td,tf->df/dot_general | solution.py:452
  394.8 14.5 %collective-permute-done.19.rb0_hbm = f32[96,3072]{1,0:T(8,128)S(1)} collective-permute-done((f32[96,3072]{1,0:T(8,128)S(1)}, f32[96,3072]{1,0:T(8,128)S(1)}, u32[]{:S(2)}, u32[]{:S(2)}) %collective-permute-start.19) | collective-permute-done | bytes 1179680 | tf_op jit(solution)/shard_map/ppermute | solution.py:51
  412.6 124.9 %tail.1 = (f32[4608,128]{1,0:T(8,128)S(1)}, f32[4608,128]{1,0:T(8,128)S(1)}, f32[4608,128]{1,0:T(8,128)S(1)}, bf16[73728,128]{1,0:T(8,128)(2,1)S(1)}) custom-call(bf16[768,1024]{1,0:T(8,128)(2,1)} %bitcast.83, bf16[768,1024]{1,0:T(8,128)(2,1)} %bitcast.81, bf16[768,1024]{1,0:T(8,128)(2,1)} %fusion.26.gd_hbm, bf16[192,1024]{1,0:T(8,128)(2,1)} %collective-permute-done.12.d0k2, ...), custom_call_target="tpu_custom_call" | custom-call | tf_op jit(solution)/shard_map/tail/pallas_call | solution.py:400
  537.5 6.7 %copy.22 = bf16[9437184]{0:T(1024)(128)(2,1)} copy(bf16[9437184]{0:T(1024)(128)(2,1)S(1)} %bitcast.74) | data formatting | bytes 37748736
  (110 shorter events, 42.5 us)
Async XLA Ops:
  0.7 54.8 %slice-start.2 = ((s8[4718592]{0:T(1024)(128)(4,1)}), s8[4194304]{0:T(1024)(128)(4,1)S(1)}, s32[]{:S(2)}) async-start(s8[4718592]{0:T(1024)(128)(4,1)} %bitcast.93), calls=%async_computation.2 | async-start | bytes 8388608
  112.7 68.0 %collective-permute-start = (bf16[768,768]{1,0:T(8,128)(2,1)}, bf16[768,768]{1,0:T(8,128)(2,1)S(1)}, u32[]{:S(2)}, u32[]{:S(2)}) collective-permute-start(bf16[768,768]{1,0:T(8,128)(2,1)} %get-tuple-element.46), channel_id=1, source_target_pairs={{0,1},{1,0},{2,3},{3,2},{4,5},{5,4},{6,7},{7,6},{8,9},{9,8},{10,11... | collective-permute-start | bytes 3538952 | tf_op jit(solution)/shard_map/ppermute | solution.py:34
  113.4 68.8 %collective-permute-start.1 = (bf16[768,768]{1,0:T(8,128)(2,1)}, bf16[768,768]{1,0:T(8,128)(2,1)S(1)}, u32[]{:S(2)}, u32[]{:S(2)}) collective-permute-start(bf16[768,768]{1,0:T(8,128)(2,1)} %get-tuple-element.48), channel_id=1, source_target_pairs={{0,2},{1,3},{2,0},{3,1},{4,6},{5,7},{6,4},{7,5},{8,10},{9,11},{10,... | collective-permute-start | bytes 3538952 | tf_op jit(solution)/shard_map/ppermute | solution.py:34
  114.6 67.6 %collective-permute-start.2 = (bf16[768,768]{1,0:T(8,128)(2,1)}, bf16[768,768]{1,0:T(8,128)(2,1)}, u32[]{:S(2)}, u32[]{:S(2)}) collective-permute-start(bf16[768,768]{1,0:T(8,128)(2,1)} %get-tuple-element.47), channel_id=1, source_target_pairs={{0,3},{1,2},{2,1},{3,0},{4,7},{5,6},{6,5},{7,4},{8,11},{9,10},{10,... | collective-permute-start | bytes 3538952 | tf_op jit(solution)/shard_map/ppermute | solution.py:34
  180.0 55.5 %collective-permute-start.3 = (bf16[192,3072]{1,0:T(8,128)(2,1)}, bf16[192,3072]{1,0:T(8,128)(2,1)}, u32[]{:S(2)}, u32[]{:S(2)}) collective-permute-start(bf16[192,3072]{1,0:T(8,128)(2,1)} %get-tuple-element.43), channel_id=1, source_target_pairs={{0,1},{1,0},{2,3},{3,2},{4,5},{5,4},{6,7},{7,6},{8,9},{9,8},{10,11... | collective-permute-start | bytes 3538952 | tf_op jit(solution)/shard_map/ppermute | solution.py:34
  180.0 56.4 %collective-permute-start.4 = (bf16[192,3072]{1,0:T(8,128)(2,1)}, bf16[192,3072]{1,0:T(8,128)(2,1)}, u32[]{:S(2)}, u32[]{:S(2)}) collective-permute-start(bf16[192,3072]{1,0:T(8,128)(2,1)} %get-tuple-element.45), channel_id=1, source_target_pairs={{0,2},{1,3},{2,0},{3,1},{4,6},{5,7},{6,4},{7,5},{8,10},{9,11},{10,... | collective-permute-start | bytes 3538952 | tf_op jit(solution)/shard_map/ppermute | solution.py:34
  180.7 56.2 %collective-permute-start.5 = (bf16[192,3072]{1,0:T(8,128)(2,1)}, bf16[192,3072]{1,0:T(8,128)(2,1)}, u32[]{:S(2)}, u32[]{:S(2)}) collective-permute-start(bf16[192,3072]{1,0:T(8,128)(2,1)} %get-tuple-element.44), channel_id=1, source_target_pairs={{0,3},{1,2},{2,1},{3,0},{4,7},{5,6},{6,5},{7,4},{8,11},{9,10},{10,... | collective-permute-start | bytes 3538952 | tf_op jit(solution)/shard_map/ppermute | solution.py:34
  209.3 79.4 %collective-permute-start.6 = (f32[768,768]{1,0:T(8,128)S(1)}, f32[768,768]{1,0:T(8,128)S(1)}, u32[]{:S(2)}, u32[]{:S(2)}) collective-permute-start(f32[768,768]{1,0:T(8,128)S(1)} %fusion.16), channel_id=1, source_target_pairs={{8,0},{9,1},{10,2},{11,3},{12,4},{13,5},{14,6},{15,7}} | collective-permute-start | bytes 7077896 | tf_op jit(solution)/shard_map/ppermute | solution.py:46
  235.0 27.8 %collective-permute-start.10 = (bf16[768,768]{1,0:T(8,128)(2,1)S(1)}, bf16[768,768]{1,0:T(8,128)(2,1)S(1)}, u32[]{:S(2)}, u32[]{:S(2)}) collective-permute-start(bf16[768,768]{1,0:T(8,128)(2,1)S(1)} %get-tuple-element.42), channel_id=1, source_target_pairs={{0,2},{1,3},{2,0},{3,1},{4,6},{5,7},{6,4},{7,5},{8,10},{9,11},{10,... | collective-permute-start | bytes 3538952 | tf_op jit(solution)/shard_map/ppermute | solution.py:34
  235.6 52.6 %collective-permute-start.11 = (bf16[768,768]{1,0:T(8,128)(2,1)S(1)}, bf16[768,768]{1,0:T(8,128)(2,1)S(1)}, u32[]{:S(2)}, u32[]{:S(2)}) collective-permute-start(bf16[768,768]{1,0:T(8,128)(2,1)S(1)} %get-tuple-element.41), channel_id=1, source_target_pairs={{0,3},{1,2},{2,1},{3,0},{4,7},{5,6},{6,5},{7,4},{8,11},{9,10},{10,... | collective-permute-start | bytes 3538952 | tf_op jit(solution)/shard_map/ppermute | solution.py:34
  236.4 51.7 %collective-permute-start.9 = (bf16[768,768]{1,0:T(8,128)(2,1)S(1)}, bf16[768,768]{1,0:T(8,128)(2,1)S(1)}, u32[]{:S(2)}, u32[]{:S(2)}) collective-permute-start(bf16[768,768]{1,0:T(8,128)(2,1)S(1)} %get-tuple-element.40), channel_id=1, source_target_pairs={{0,1},{1,0},{2,3},{3,2},{4,5},{5,4},{6,7},{7,6},{8,9},{9,8},{10,11... | collective-permute-start | bytes 3538952 | tf_op jit(solution)/shard_map/ppermute | solution.py:34
  290.3 39.6 %collective-permute-start.7 = (f32[96,3072]{1,0:T(8,128)}, f32[96,3072]{1,0:T(8,128)S(1)}, u32[]{:S(2)}, u32[]{:S(2)}) collective-permute-start(f32[96,3072]{1,0:T(8,128)} %get-tuple-element.52), channel_id=1, source_target_pairs={{12,4},{13,5},{14,6},{15,7},{8,0},{9,1},{10,2},{11,3}} | collective-permute-start | bytes 3538952 | tf_op jit(solution)/shard_map/ppermute | solution.py:46
  291.7 38.2 %collective-permute-start.8 = (f32[96,3072]{1,0:T(8,128)S(1)}, f32[96,3072]{1,0:T(8,128)}, u32[]{:S(2)}, u32[]{:S(2)}) collective-permute-start(f32[96,3072]{1,0:T(8,128)S(1)} %get-tuple-element.51), channel_id=1, source_target_pairs={{0,4},{1,5},{2,6},{3,7},{8,12},{9,13},{10,14},{11,15}} | collective-permute-start | bytes 3538952 | tf_op jit(solution)/shard_map/ppermute | solution.py:51
  293.0 117.3 %collective-permute-start.18 = (f32[768,768]{1,0:T(8,128)S(1)}, f32[768,768]{1,0:T(8,128)S(1)}, u32[]{:S(2)}, u32[]{:S(2)}) collective-permute-start(f32[768,768]{1,0:T(8,128)S(1)} %add.91.qa_hbm), channel_id=1, source_target_pairs={{4,0},{5,1},{6,2},{7,3}} | collective-permute-start | bytes 7077896 | tf_op jit(solution)/shard_map/ppermute | solution.py:51
  343.5 14.1 %collective-permute-start.15 = (bf16[192,1024]{1,0:T(8,128)(2,1)S(1)}, bf16[192,1024]{1,0:T(8,128)(2,1)S(1)}, u32[]{:S(2)}, u32[]{:S(2)}) collective-permute-start(bf16[192,1024]{1,0:T(8,128)(2,1)S(1)} %get-tuple-element.55), channel_id=1, source_target_pairs={{0,2},{1,3},{2,0},{3,1},{4,6},{5,7},{6,4},{7,5},{8,10},{9,11},{10,... | collective-permute-start | bytes 1179656 | tf_op jit(solution)/shard_map/ppermute | solution.py:34
  343.9 20.3 %collective-permute-start.16 = (bf16[192,1024]{1,0:T(8,128)(2,1)S(1)}, bf16[192,1024]{1,0:T(8,128)(2,1)S(1)}, u32[]{:S(2)}, u32[]{:S(2)}) collective-permute-start(bf16[192,1024]{1,0:T(8,128)(2,1)S(1)} %get-tuple-element.54), channel_id=1, source_target_pairs={{0,3},{1,2},{2,1},{3,0},{4,7},{5,6},{6,5},{7,4},{8,11},{9,10},{10,... | collective-permute-start | bytes 1179656 | tf_op jit(solution)/shard_map/ppermute | solution.py:34
  357.1 8.0 %collective-permute-start.17 = (bf16[192,1024]{1,0:T(8,128)(2,1)S(1)}, bf16[192,1024]{1,0:T(8,128)(2,1)S(1)}, u32[]{:S(2)}, u32[]{:S(2)}) collective-permute-start(bf16[192,1024]{1,0:T(8,128)(2,1)S(1)} %get-tuple-element.53), channel_id=1, source_target_pairs={{0,1},{1,0},{2,3},{3,2},{4,5},{5,4},{6,7},{7,6},{8,9},{9,8},{10,11... | collective-permute-start | bytes 1179656 | tf_op jit(solution)/shard_map/ppermute | solution.py:34
  357.3 12.9 %collective-permute-start.12 = (bf16[192,1024]{1,0:T(8,128)(2,1)S(1)}, bf16[192,1024]{1,0:T(8,128)(2,1)}, u32[]{:S(2)}, u32[]{:S(2)}) collective-permute-start(bf16[192,1024]{1,0:T(8,128)(2,1)S(1)} %get-tuple-element.58), channel_id=1, source_target_pairs={{0,2},{1,3},{2,0},{3,1},{4,6},{5,7},{6,4},{7,5},{8,10},{9,11},{10,... | collective-permute-start | bytes 1179656 | tf_op jit(solution)/shard_map/ppermute | solution.py:34
  357.6 22.0 %collective-permute-start.13 = (bf16[192,1024]{1,0:T(8,128)(2,1)S(1)}, bf16[192,1024]{1,0:T(8,128)(2,1)S(1)}, u32[]{:S(2)}, u32[]{:S(2)}) collective-permute-start(bf16[192,1024]{1,0:T(8,128)(2,1)S(1)} %get-tuple-element.57), channel_id=1, source_target_pairs={{0,3},{1,2},{2,1},{3,0},{4,7},{5,6},{6,5},{7,4},{8,11},{9,10},{10,... | collective-permute-start | bytes 1179656 | tf_op jit(solution)/shard_map/ppermute | solution.py:34
  364.9 16.0 %collective-permute-start.14 = (bf16[192,1024]{1,0:T(8,128)(2,1)S(1)}, bf16[192,1024]{1,0:T(8,128)(2,1)S(1)}, u32[]{:S(2)}, u32[]{:S(2)}) collective-permute-start(bf16[192,1024]{1,0:T(8,128)(2,1)S(1)} %get-tuple-element.56), channel_id=1, source_target_pairs={{0,1},{1,0},{2,3},{3,2},{4,5},{5,4},{6,7},{7,6},{8,9},{9,8},{10,11... | collective-permute-start | bytes 1179656 | tf_op jit(solution)/shard_map/ppermute | solution.py:34
  365.2 45.2 %collective-permute-start.21 = (f32[480,768]{1,0:T(8,128)S(1)}, f32[480,768]{1,0:T(8,128)S(1)}, u32[]{:S(2)}, u32[]{:S(2)}) collective-permute-start(f32[480,768]{1,0:T(8,128)S(1)} %slice.26.pc0_hbm), channel_id=1, source_target_pairs={{0,8},{1,9},{2,10},{3,11},{4,12},{5,13},{6,14},{7,15}} | collective-permute-start | bytes 4423688 | tf_op jit(solution)/shard_map/ppermute | solution.py:46
  370.2 24.6 %collective-permute-start.22 = (f32[288,768]{1,0:T(8,128)S(1)}, f32[288,768]{1,0:T(8,128)S(1)}, u32[]{:S(2)}, u32[]{:S(2)}) collective-permute-start(f32[288,768]{1,0:T(8,128)S(1)} %slice.27.pc1_hbm), channel_id=1, source_target_pairs={{12,8},{13,9},{14,10},{15,11},{4,0},{5,1},{6,2},{7,3}} | collective-permute-start | bytes 2654216 | tf_op jit(solution)/shard_map/ppermute | solution.py:51
  379.6 29.6 %collective-permute-start.19 = (f32[96,3072]{1,0:T(8,128)S(1)}, f32[96,3072]{1,0:T(8,128)S(1)}, u32[]{:S(2)}, u32[]{:S(2)}) collective-permute-start(f32[96,3072]{1,0:T(8,128)S(1)} %get-tuple-element.33.qb0_hbm), channel_id=1, source_target_pairs={{0,4},{1,5},{2,6},{3,7}} | collective-permute-start | bytes 3538952 | tf_op jit(solution)/shard_map/ppermute | solution.py:51
  381.0 29.3 %collective-permute-start.20 = (f32[96,3072]{1,0:T(8,128)S(1)}, f32[96,3072]{1,0:T(8,128)S(1)}, u32[]{:S(2)}, u32[]{:S(2)}) collective-permute-start(f32[96,3072]{1,0:T(8,128)S(1)} %get-tuple-element.34.qb1_hbm), channel_id=1, source_target_pairs={{12,4},{13,5},{14,6},{15,7}} | collective-permute-start | bytes 3538952 | tf_op jit(solution)/shard_map/ppermute | solution.py:46
  (27 other events, 483.8 us)

commit v4 on v3

--- a/solution.py
+++ b/solution.py
@@ -73,24 +73,26 @@
 SHARD_ROWS = 4608
 N_PIECE = 6
 PIECE_ROWS = SHARD_ROWS // N_PIECE
-CH_COLS = 512
-N_CH = 6
-N_PRE = 4
+CH_COLS = 256
+N_CH = 12
+N_PRE = 8
 PIECE_COLS = 1024
 X_BIT, Y_BIT, Z_BIT = 1, 2, 4
 ADAM_ROWS = 96
-C_TOP = 480
+C_TOP = 528
+D_TOP = 80
 ORDERS = ((X_BIT, Y_BIT, Z_BIT), (Y_BIT, Z_BIT, X_BIT), (Z_BIT, X_BIT, Y_BIT)) * 2
 
 
 def tail_kernel(gd0_hbm, gd1_hbm, gd_hbm, d0k2, d0k3, d0k1, d1k2, d1k3, d1k1,
                 qa_hbm, ra_hbm, qb0_hbm, qb1_hbm, rb0_hbm, rb1_hbm, pc0_hbm, pc1_hbm, rc0_hbm, rc1_hbm,
                 mst_hbm, m_hbm, v_hbm, omst_hbm, om_hbm, ov_hbm, w_hbm,
-                own, xrecv, part, a1, b1, a2, b2, sq_a, sq_b, c_a, c_b, wide_a, wide_b, s_v, mst_v, m_v, v_v, w_v,
+                own, xrecv, part, top_got, bot_got, sq_a, sq_b, c_a, c_b, wide_a, wide_b, s_v, mst_v, m_v, v_v, w_v,
                 ld_sem, st_sem, c_send, c_recv, xs_send, xs_recv, yz_send, yz_recv, ag_send, ag_recv, dd_send, dd_recv):
     z, y, x = (lax.axis_index(a) for a in AXES)
     ny, nz = 1 - y, 1 - z
     is_late = (z == 1) & (y == 1)
+    is_a, is_b, is_c = (z == 0) & (y == 0), (z == 0) & (y == 1), (z == 1) & (y == 0)
     f32 = jnp.float32
 
     def x_peer(k):
@@ -135,7 +137,6 @@
     loads = [pltpu.make_async_copy(src, dst, ld_sem.at[i]) for i, (src, dst) in enumerate(pre + state)]
     for cp in loads:
         cp.start()
-    is_a, is_b, is_c = (z == 0) & (y == 0), (z == 0) & (y == 1), (z == 1) & (y == 0)
 
     def fetch(items, base=12):
         return [pltpu.make_async_copy(src, dst, ld_sem.at[base + i]) for i, (src, dst) in enumerate(items)]
@@ -190,35 +191,35 @@
     for cp in loads[:len(pre)]:
         cp.wait()
 
-    top, bot = pl.ds(0, 96), pl.ds(96, 96)
+    top, bot = pl.ds(0, D_TOP), pl.ds(D_TOP, 192 - D_TOP)
+    chain = ((top, top_got, Y_BIT, is_b, is_a), (top, top_got, Z_BIT, is_a, is_c), (top, top_got, Y_BIT, is_c, is_late),
+             (bot, bot_got, Z_BIT, is_c, is_a), (bot, bot_got, Y_BIT, is_a, is_b), (bot, bot_got, Z_BIT, is_b, is_late))
 
     def yz_copy(kind, ch):
-        rows, dst, where = ((top, a1, peers[Z_BIT]), (bot, b1, peers[Y_BIT]),
-                            (top, a2, peers[Y_BIT]), (bot, b2, peers[Z_BIT]))[kind]
+        rows, dst, bit = chain[kind][:3]
         return remote(part.at[rows, cols(ch)], dst.at[:, cols(ch)],
-                      yz_send.at[kind, ch], yz_recv.at[kind, ch], where)
-
-    yz_sends = {0: z == 0, 1: y == 0, 2: (z == 1) & (y == 0), 3: (z == 0) & (y == 1)}
-    yz_takes = {0: z == 1, 1: y == 1, 2: is_late, 3: is_late}
-
-    def yz_start(kind, ch):
-        @pl.when(yz_sends[kind])
-        def _():
-            yz_copy(kind, ch).start()
-
-    def yz_take(kind, ch):
-        @pl.when(yz_takes[kind])
-        def _():
-            yz_copy(kind, ch).wait_recv()
-            got = (a1, b1, a2, b2)[kind]
-            base = 0 if kind in (0, 2) else 96
-
-            def body(i, _):
-                rows = pl.ds(pl.multiple_of(base + i * 8, 8), 8)
-                part[rows, cols(ch)] += got[pl.ds(pl.multiple_of(i * 8, 8), 8), cols(ch)]
-                return 0
-
-            lax.fori_loop(0, 12, body, 0)
+                      yz_send.at[kind, ch], yz_recv.at[kind, ch], peers[bit])
+
+    def yz_start(kinds, ch):
+        for kind in kinds:
+            @pl.when(chain[kind][3])
+            def _():
+                yz_copy(kind, ch).start()
+
+    def yz_take(kinds, ch):
+        for kind in kinds:
+            @pl.when(chain[kind][4])
+            def _():
+                yz_copy(kind, ch).wait_recv()
+                got = chain[kind][1]
+                base, count = (0, D_TOP) if kind < 3 else (D_TOP, 192 - D_TOP)
+
+                def body(i, _):
+                    rows = pl.ds(pl.multiple_of(base + i * 8, 8), 8)
+                    part[rows, cols(ch)] += got[pl.ds(pl.multiple_of(i * 8, 8), 8), cols(ch)]
+                    return 0
+
+                lax.fori_loop(0, count // 8, body, 0)
 
     def x_sum(ch):
         if ch >= N_PRE:
@@ -300,8 +301,7 @@
 
     for ch in range(N_PRE):
         x_sum(ch)
-        yz_start(0, ch)
-        yz_start(1, ch)
+        yz_start((0, 3), ch)
     for cp in loads[len(pre):]:
         cp.wait()
 
@@ -325,30 +325,30 @@
             own_update()
 
     for ch in range(N_PRE):
-        yz_take(0, ch)
-        yz_take(1, ch)
-        yz_start(2, ch)
-        yz_start(3, ch)
+        yz_take((0, 3), ch)
+        yz_start((1, 4), ch)
+
+    @pl.when(is_a)
+    def _():
+        c_copy(1).start()
+
     for ch in range(N_PRE, N_CH):
         x_sum(ch)
-        yz_start(0, ch)
-        yz_start(1, ch)
-        if ch == N_PRE:
-            @pl.when(is_a)
-            def _():
-                c_copy(1).start()
+        yz_start((0, 3), ch)
+    for ch in range(N_PRE):
+        yz_take((1, 4), ch)
+        yz_start((2, 5), ch)
     for ch in range(N_PRE, N_CH):
-        yz_take(0, ch)
-        yz_take(1, ch)
-        yz_start(2, ch)
-        yz_start(3, ch)
+        yz_take((0, 3), ch)
+        yz_start((1, 4), ch)
+    for ch in range(N_PRE, N_CH):
+        yz_take((1, 4), ch)
+        yz_start((2, 5), ch)
 
     @pl.when(is_late)
     def _():
         for ch in range(N_CH):
-            for kind in (2, 3):
-                yz_take(kind, ch)
-
+            yz_take((2, 5), ch)
         spread((part,), 24, 24)
         own_update()
 
@@ -378,8 +378,8 @@
         for k in (1, 2, 3):
             xs_copy(k, ch).wait_send()
     for ch in range(N_CH):
-        for kind in range(4):
-            @pl.when(yz_sends[kind])
+        for kind in range(6):
+            @pl.when(chain[kind][3])
             def _():
                 yz_copy(kind, ch).wait_send()
     for kind in (0, 1):
@@ -395,7 +395,6 @@
     f32, bf16 = jnp.float32, jnp.bfloat16
     dma = pltpu.SemaphoreType.DMA
     shard = pltpu.VMEM((SHARD_ROWS, 128), f32)
-    half = pltpu.VMEM((96, 3072), f32)
     square = pltpu.VMEM((768, 768), f32)
     return pl.pallas_call(
         tail_kernel,
@@ -404,11 +403,11 @@
         out_specs=[any_spec] * 4,
         scratch_shapes=[
             pltpu.VMEM((192, 3072), bf16), pltpu.VMEM((3, 192, 3072), bf16), pltpu.VMEM((192, 3072), f32),
-            half, half, half, half, square, square, square, square,
+            pltpu.VMEM((D_TOP, 3072), f32), pltpu.VMEM((192 - D_TOP, 3072), f32), square, square, square, square,
             pltpu.VMEM((192, 3072), f32), pltpu.VMEM((192, 3072), f32),
             shard, shard, shard, shard, pltpu.VMEM((SHARD_ROWS, 128), bf16),
             dma((18,)), dma((4,)), dma((2,)), dma((2,)),
-            dma((3, N_CH - N_PRE)), dma((3, N_CH - N_PRE)), dma((4, N_CH)), dma((4, N_CH)),
+            dma((3, N_CH - N_PRE)), dma((3, N_CH - N_PRE)), dma((6, N_CH)), dma((6, N_CH)),
             dma((N_PIECE, 3, 8)), dma((N_PIECE, 8)), dma((N_PIECE, 8)), dma((N_PIECE, 8)),
         ],
         compiler_params=pltpu.CompilerParams(collective_id=0, has_side_effects=True, vmem_limit_bytes=38 << 20),

time: 556 us -> 552 us (level)
  the two profiles are of different devices: /device:TPU:5 before, /device:TPU:0 now
where the time goes in v4:
time: 552 us; the launch traced here: 544 us
  matrix products  217 us (39%)
  Pallas kernels  184 us (33%)
  waiting for transfers between devices  74.1 us (13%)
  starting transfers between devices  32.5 us (6%)
  local copies, waits for them, and re-layouts  27 us (5%)
  other arithmetic  7.64 us (1%)
    dot_general x10, matrix products, mm(): return jnp.einsum(spec, a, b, preferred_element_type=f32)  217 us
    pallas_call x1, Pallas kernels, tail(): pl.pallas_call(tail_kernel, out_shape=(shard, shard, shard, pltpu.VMEM((1...  121 us
    pallas_call x2, Pallas kernels, slope_product(): pl.pallas_call(kernel, grid=(full // cols, tokens // rows), in_specs=[pl....  63 us
    ppermute x15, waiting for transfers between devices, send_x(): got.append(lax.ppermute(send, 'dpx', [(i, i ^ k) for i in range(4)]))  61.3 us
    unnamed x62, local copies, waits for them, and re-layouts  21.4 us
    ppermute x15, starting transfers between devices, send_x(): got.append(lax.ppermute(send, 'dpx', [(i, i ^ k) for i in range(4)]))  13.5 us
    ppermute x4, waiting for transfers between devices, shift_y(): return lax.ppermute(val, AXES, pairs)  12.8 us
    ppermute x4, starting transfers between devices, shift_y(): return lax.ppermute(val, AXES, pairs)  11.3 us
  transfers between devices with their start and end apart: 23, of which 6 were waited for; matrix products, arithmetic and copies ran while one was open for 22% of the time, Pallas kernels for 12%

profile of v4, /device:TPU:0, one launch (start us, length us, event | category | flops | bytes accessed | tf_op | source)
XLA Modules:
  0.0 544.0 jit_solution(6342137554387530278)
XLA Ops:
  0.7 30.3 %fusion.1 = (bf16[4096,3072]{1,0:T(8,128)(2,1)}, bf16[4096,3072]{1,0:T(8,128)(2,1)}) fusion(bf16[4096,768]{1,0:T(8,128)(2,1)} %param.9, bf16[768,3072]{1,0:T(8,128)(2,1)} %param.11), kind=kOutput, calls=%fused_computation.5 | convolution fusion | flops 19415433216 | bytes 61341696 | tf_op jit(solution)/shard_map/td,df->tf/dot_general | solution.py:451
  31.0 24.4 %add_convert_fusion.1 = bf16[4096,768]{1,0:T(8,128)(2,1)} fusion(bf16[4096,768]{1,0:T(8,128)(2,1)S(1)} %copy-done.23, bf16[4096,3072]{1,0:T(8,128)(2,1)} %get-tuple-element.22, bf16[3072,768]{1,0:T(8,128)(2,1)S(1)} %copy-done.2), kind=kOutput, calls=%fused_computation.15 | convolution fusion | flops 19336790016 | bytes 42467328 | tf_op jit(solution)/shard_map/tf,fd->td/dot_general | solution.py:451
  55.5 29.3 %fusion.5 = (bf16[4096,3072]{1,0:T(8,128)(2,1)}, bf16[4096,3072]{1,0:T(8,128)(2,1)}) fusion(bf16[4096,768]{1,0:T(8,128)(2,1)} %add_convert_fusion.1, bf16[768,3072]{1,0:T(8,128)(2,1)S(1)} %bitcast.94), kind=kOutput, calls=%fused_computation.9 | convolution fusion | flops 19415433216 | bytes 61341696 | tf_op jit(solution)/shard_map/td,df->tf/dot_general | solution.py:451
  84.8 25.3 %convolution_convert_fusion.4 = bf16[3072,768]{1,0:T(8,128)(2,1)S(1)} fusion(bf16[4096,3072]{1,0:T(8,128)(2,1)} %get-tuple-element.24, bf16[4096,768]{1,0:T(8,128)(2,1)} %grad_ref.1), kind=kOutput, calls=%fused_computation.24 | convolution fusion | flops 19329712128 | bytes 36175872 | tf_op jit(solution)/shard_map/tf,td->fd/dot_general | solution.py:451
  121.1 31.3 %slope_product.2 = bf16[4096,3072]{1,0:T(8,128)(2,1)} custom-call(bf16[4096,768]{1,0:T(8,128)(2,1)S(1)} %copy-done, bf16[3072,768]{1,0:T(8,128)(2,1)S(1)} %copy-done.1, bf16[4096,3072]{1,0:T(8,128)(2,1)} %get-tuple-element.23.pre_ref), custom_call_target="tpu_custom_call" | custom-call | flops 19327352832 | bytes 50331648 | tf_op jit(solution)/shard_map/slope_product/pallas_call | solution.py:430
  152.4 23.5 %convolution_convert_fusion.3 = bf16[768,3072]{1,0:T(8,128)(2,1)S(1)} fusion(bf16[4096,768]{1,0:T(8,128)(2,1)S(1)} %copy-done.24, bf16[4096,3072]{1,0:T(8,128)(2,1)} %slope_product.2), kind=kOutput, calls=%fused_computation.23 | convolution fusion | flops 19329712128 | bytes 36175872 | tf_op jit(solution)/shard_map/td,tf->df/dot_general | solution.py:451
  184.2 25.0 %add_convert_fusion.grad_ref = bf16[4096,768]{1,0:T(8,128)(2,1)S(1)} fusion(bf16[4096,768]{1,0:T(8,128)(2,1)} %grad_ref.1, bf16[4096,3072]{1,0:T(8,128)(2,1)} %slope_product.2, bf16[768,3072]{1,0:T(8,128)(2,1)} %param.13), kind=kOutput, calls=%fused_computation.14 | convolution fusion | flops 19336790016 | bytes 42467328 | tf_op jit(solution)/shard_map/tf,df->td/dot_general | solution.py:451
  210.5 24.1 %convolution_convert_fusion.2 = bf16[3072,768]{1,0:T(8,128)(2,1)S(1)} fusion(bf16[4096,3072]{1,0:T(8,128)(2,1)} %get-tuple-element.22, bf16[4096,768]{1,0:T(8,128)(2,1)S(1)} %add_convert_fusion.grad_ref), kind=kOutput, calls=%fused_computation.22 | convolution fusion | flops 19329712128 | bytes 36175872 | tf_op jit(solution)/shard_map/tf,td->fd/dot_general | solution.py:451
  237.0 3.1 fusion.15
  240.1 23.6 %collective-permute-done.10 = bf16[768,768]{1,0:T(8,128)(2,1)S(1)} collective-permute-done((bf16[768,768]{1,0:T(8,128)(2,1)S(1)}, bf16[768,768]{1,0:T(8,128)(2,1)S(1)}, u32[]{:S(2)}, u32[]{:S(2)}) %collective-permute-start.10) | collective-permute-done | bytes 1179680 | tf_op jit(solution)/shard_map/ppermute | solution.py:34
  263.7 24.9 %collective-permute-done.11 = bf16[768,768]{1,0:T(8,128)(2,1)S(1)} collective-permute-done((bf16[768,768]{1,0:T(8,128)(2,1)S(1)}, bf16[768,768]{1,0:T(8,128)(2,1)S(1)}, u32[]{:S(2)}, u32[]{:S(2)}) %collective-permute-start.11) | collective-permute-done | bytes 1179680 | tf_op jit(solution)/shard_map/ppermute | solution.py:34
  292.1 4.5 collective-permute-start.8
  297.9 31.7 %slope_product.3 = bf16[4096,3072]{1,0:T(8,128)(2,1)} custom-call(bf16[4096,768]{1,0:T(8,128)(2,1)S(1)} %add_convert_fusion.grad_ref, bf16[3072,768]{1,0:T(8,128)(2,1)S(1)} %bitcast.79, bf16[4096,3072]{1,0:T(8,128)(2,1)} %get-tuple-element.28.pre_ref), custom_call_target="tpu_custom_call" | custom-call | flops 19327352832 | bytes 50331648 | tf_op jit(solution)/shard_map/slope_product/pallas_call | solution.py:430
  331.3 11.8 %fusion.20 = bf16[1024,768]{0,1:T(8,128)(2,1)S(1)} fusion(bf16[4096,768]{1,0:T(8,128)(2,1)} %param.9, bf16[4096,3072]{1,0:T(8,128)(2,1)} %slope_product.3), kind=kOutput, calls=%fused_computation.32 | convolution fusion | flops 6443237376 | bytes 16252928 | tf_op jit(solution)/shard_map/td,tf->df/dot_general | solution.py:451
  344.5 11.0 %fusion.17 = bf16[1024,768]{0,1:T(8,128)(2,1)S(1)} fusion(bf16[4096,768]{1,0:T(8,128)(2,1)} %param.9, bf16[4096,3072]{1,0:T(8,128)(2,1)} %slope_product.3), kind=kOutput, calls=%fused_computation.31 | convolution fusion | flops 6443237376 | bytes 16252928 | tf_op jit(solution)/shard_map/td,tf->df/dot_general | solution.py:451
  358.0 3.7 collective-permute-done.16.d1k3
  363.7 4.2 collective-permute-start.21
  367.9 4.2 collective-permute-done.12.d0k2
  373.4 4.8 collective-permute-done.13.d0k3
  378.3 4.2 collective-permute-start.19
  383.3 12.4 %fusion.26.gd_hbm = bf16[768,1024]{1,0:T(8,128)(2,1)} fusion(bf16[4096,768]{1,0:T(8,128)(2,1)} %param.9, bf16[4096,3072]{1,0:T(8,128)(2,1)} %slope_product.3), kind=kOutput, calls=%fused_computation.34 | convolution fusion | flops 6443237376 | bytes 16252928 | tf_op jit(solution)/shard_map/td,tf->df/dot_general | solution.py:451
  395.7 12.8 %collective-permute-done.19.rb0_hbm = f32[96,3072]{1,0:T(8,128)S(1)} collective-permute-done((f32[96,3072]{1,0:T(8,128)S(1)}, f32[96,3072]{1,0:T(8,128)S(1)}, u32[]{:S(2)}, u32[]{:S(2)}) %collective-permute-start.19) | collective-permute-done | bytes 1179680 | tf_op jit(solution)/shard_map/ppermute | solution.py:51
  411.2 121.2 %tail.1 = (f32[4608,128]{1,0:T(8,128)S(1)}, f32[4608,128]{1,0:T(8,128)S(1)}, f32[4608,128]{1,0:T(8,128)S(1)}, bf16[73728,128]{1,0:T(8,128)(2,1)S(1)}) custom-call(bf16[768,1024]{1,0:T(8,128)(2,1)} %bitcast.83, bf16[768,1024]{1,0:T(8,128)(2,1)} %bitcast.81, bf16[768,1024]{1,0:T(8,128)(2,1)} %fusion.26.gd_hbm, bf16[192,1024]{1,0:T(8,128)(2,1)} %copy-done.20, ...), custom_call_target="tpu_custom_call" | custom-call | tf_op jit(solution)/shard_map/tail/pallas_call | solution.py:399
  532.4 6.7 %copy.22 = bf16[9437184]{0:T(1024)(128)(2,1)} copy(bf16[9437184]{0:T(1024)(128)(2,1)S(1)} %bitcast.74) | data formatting | bytes 37748736
  (112 shorter events, 44.5 us)
Async XLA Ops:
  0.7 54.8 %slice-start.2 = ((s8[4718592]{0:T(1024)(128)(4,1)}), s8[4194304]{0:T(1024)(128)(4,1)S(1)}, s32[]{:S(2)}) async-start(s8[4718592]{0:T(1024)(128)(4,1)} %bitcast.93), calls=%async_computation.2 | async-start | bytes 8388608
  112.0 69.4 %collective-permute-start = (bf16[768,768]{1,0:T(8,128)(2,1)}, bf16[768,768]{1,0:T(8,128)(2,1)S(1)}, u32[]{:S(2)}, u32[]{:S(2)}) collective-permute-start(bf16[768,768]{1,0:T(8,128)(2,1)} %get-tuple-element.46), channel_id=1, source_target_pairs={{0,1},{1,0},{2,3},{3,2},{4,5},{5,4},{6,7},{7,6},{8,9},{9,8},{10,11... | collective-permute-start | bytes 3538952 | tf_op jit(solution)/shard_map/ppermute | solution.py:34
  112.8 69.3 %collective-permute-start.1 = (bf16[768,768]{1,0:T(8,128)(2,1)}, bf16[768,768]{1,0:T(8,128)(2,1)S(1)}, u32[]{:S(2)}, u32[]{:S(2)}) collective-permute-start(bf16[768,768]{1,0:T(8,128)(2,1)} %get-tuple-element.48), channel_id=1, source_target_pairs={{0,2},{1,3},{2,0},{3,1},{4,6},{5,7},{6,4},{7,5},{8,10},{9,11},{10,... | collective-permute-start | bytes 3538952 | tf_op jit(solution)/shard_map/ppermute | solution.py:34
  115.3 66.8 %collective-permute-start.2 = (bf16[768,768]{1,0:T(8,128)(2,1)}, bf16[768,768]{1,0:T(8,128)(2,1)}, u32[]{:S(2)}, u32[]{:S(2)}) collective-permute-start(bf16[768,768]{1,0:T(8,128)(2,1)} %get-tuple-element.47), channel_id=1, source_target_pairs={{0,3},{1,2},{2,1},{3,0},{4,7},{5,6},{6,5},{7,4},{8,11},{9,10},{10,... | collective-permute-start | bytes 3538952 | tf_op jit(solution)/shard_map/ppermute | solution.py:34
  180.0 55.8 %collective-permute-start.3 = (bf16[192,3072]{1,0:T(8,128)(2,1)}, bf16[192,3072]{1,0:T(8,128)(2,1)}, u32[]{:S(2)}, u32[]{:S(2)}) collective-permute-start(bf16[192,3072]{1,0:T(8,128)(2,1)} %get-tuple-element.43), channel_id=1, source_target_pairs={{0,1},{1,0},{2,3},{3,2},{4,5},{5,4},{6,7},{7,6},{8,9},{9,8},{10,11... | collective-permute-start | bytes 3538952 | tf_op jit(solution)/shard_map/ppermute | solution.py:34
  180.7 56.3 %collective-permute-start.4 = (bf16[192,3072]{1,0:T(8,128)(2,1)}, bf16[192,3072]{1,0:T(8,128)(2,1)}, u32[]{:S(2)}, u32[]{:S(2)}) collective-permute-start(bf16[192,3072]{1,0:T(8,128)(2,1)} %get-tuple-element.45), channel_id=1, source_target_pairs={{0,2},{1,3},{2,0},{3,1},{4,6},{5,7},{6,4},{7,5},{8,10},{9,11},{10,... | collective-permute-start | bytes 3538952 | tf_op jit(solution)/shard_map/ppermute | solution.py:34
  181.4 55.6 %collective-permute-start.5 = (bf16[192,3072]{1,0:T(8,128)(2,1)}, bf16[192,3072]{1,0:T(8,128)(2,1)}, u32[]{:S(2)}, u32[]{:S(2)}) collective-permute-start(bf16[192,3072]{1,0:T(8,128)(2,1)} %get-tuple-element.44), channel_id=1, source_target_pairs={{0,3},{1,2},{2,1},{3,0},{4,7},{5,6},{6,5},{7,4},{8,11},{9,10},{10,... | collective-permute-start | bytes 3538952 | tf_op jit(solution)/shard_map/ppermute | solution.py:34
  209.2 80.0 %collective-permute-start.6 = (f32[768,768]{1,0:T(8,128)S(1)}, f32[768,768]{1,0:T(8,128)S(1)}, u32[]{:S(2)}, u32[]{:S(2)}) collective-permute-start(f32[768,768]{1,0:T(8,128)S(1)} %fusion.16), channel_id=1, source_target_pairs={{8,0},{9,1},{10,2},{11,3},{12,4},{13,5},{14,6},{15,7}} | collective-permute-start | bytes 7077896 | tf_op jit(solution)/shard_map/ppermute | solution.py:46
  234.8 28.9 %collective-permute-start.10 = (bf16[768,768]{1,0:T(8,128)(2,1)S(1)}, bf16[768,768]{1,0:T(8,128)(2,1)S(1)}, u32[]{:S(2)}, u32[]{:S(2)}) collective-permute-start(bf16[768,768]{1,0:T(8,128)(2,1)S(1)} %get-tuple-element.42), channel_id=1, source_target_pairs={{0,2},{1,3},{2,0},{3,1},{4,6},{5,7},{6,4},{7,5},{8,10},{9,11},{10,... | collective-permute-start | bytes 3538952 | tf_op jit(solution)/shard_map/ppermute | solution.py:34
  235.8 52.8 %collective-permute-start.11 = (bf16[768,768]{1,0:T(8,128)(2,1)S(1)}, bf16[768,768]{1,0:T(8,128)(2,1)S(1)}, u32[]{:S(2)}, u32[]{:S(2)}) collective-permute-start(bf16[768,768]{1,0:T(8,128)(2,1)S(1)} %get-tuple-element.41), channel_id=1, source_target_pairs={{0,3},{1,2},{2,1},{3,0},{4,7},{5,6},{6,5},{7,4},{8,11},{9,10},{10,... | collective-permute-start | bytes 3538952 | tf_op jit(solution)/shard_map/ppermute | solution.py:34
  237.0 51.6 %collective-permute-start.9 = (bf16[768,768]{1,0:T(8,128)(2,1)S(1)}, bf16[768,768]{1,0:T(8,128)(2,1)S(1)}, u32[]{:S(2)}, u32[]{:S(2)}) collective-permute-start(bf16[768,768]{1,0:T(8,128)(2,1)S(1)} %get-tuple-element.40), channel_id=1, source_target_pairs={{0,1},{1,0},{2,3},{3,2},{4,5},{5,4},{6,7},{7,6},{8,9},{9,8},{10,11... | collective-permute-start | bytes 3538952 | tf_op jit(solution)/shard_map/ppermute | solution.py:34
  290.7 38.9 %collective-permute-start.7 = (f32[96,3072]{1,0:T(8,128)}, f32[96,3072]{1,0:T(8,128)S(1)}, u32[]{:S(2)}, u32[]{:S(2)}) collective-permute-start(f32[96,3072]{1,0:T(8,128)} %get-tuple-element.52), channel_id=1, source_target_pairs={{12,4},{13,5},{14,6},{15,7},{8,0},{9,1},{10,2},{11,3}} | collective-permute-start | bytes 3538952 | tf_op jit(solution)/shard_map/ppermute | solution.py:46
  292.1 37.5 %collective-permute-start.8 = (f32[96,3072]{1,0:T(8,128)S(1)}, f32[96,3072]{1,0:T(8,128)}, u32[]{:S(2)}, u32[]{:S(2)}) collective-permute-start(f32[96,3072]{1,0:T(8,128)S(1)} %get-tuple-element.51), channel_id=1, source_target_pairs={{0,4},{1,5},{2,6},{3,7},{8,12},{9,13},{10,14},{11,15}} | collective-permute-start | bytes 3538952 | tf_op jit(solution)/shard_map/ppermute | solution.py:51
  296.6 111.9 %collective-permute-start.18 = (f32[768,768]{1,0:T(8,128)S(1)}, f32[768,768]{1,0:T(8,128)S(1)}, u32[]{:S(2)}, u32[]{:S(2)}) collective-permute-start(f32[768,768]{1,0:T(8,128)S(1)} %add.91.qa_hbm), channel_id=1, source_target_pairs={{4,0},{5,1},{6,2},{7,3}} | collective-permute-start | bytes 7077896 | tf_op jit(solution)/shard_map/ppermute | solution.py:51
  343.2 13.9 %collective-permute-start.15 = (bf16[192,1024]{1,0:T(8,128)(2,1)S(1)}, bf16[192,1024]{1,0:T(8,128)(2,1)S(1)}, u32[]{:S(2)}, u32[]{:S(2)}) collective-permute-start(bf16[192,1024]{1,0:T(8,128)(2,1)S(1)} %get-tuple-element.55), channel_id=1, source_target_pairs={{0,2},{1,3},{2,0},{3,1},{4,6},{5,7},{6,4},{7,5},{8,10},{9,11},{10,... | collective-permute-start | bytes 1179656 | tf_op jit(solution)/shard_map/ppermute | solution.py:34
  343.8 17.9 %collective-permute-start.16 = (bf16[192,1024]{1,0:T(8,128)(2,1)S(1)}, bf16[192,1024]{1,0:T(8,128)(2,1)S(1)}, u32[]{:S(2)}, u32[]{:S(2)}) collective-permute-start(bf16[192,1024]{1,0:T(8,128)(2,1)S(1)} %get-tuple-element.54), channel_id=1, source_target_pairs={{0,3},{1,2},{2,1},{3,0},{4,7},{5,6},{6,5},{7,4},{8,11},{9,10},{10,... | collective-permute-start | bytes 1179656 | tf_op jit(solution)/shard_map/ppermute | solution.py:34
  355.5 8.2 %collective-permute-start.17 = (bf16[192,1024]{1,0:T(8,128)(2,1)S(1)}, bf16[192,1024]{1,0:T(8,128)(2,1)S(1)}, u32[]{:S(2)}, u32[]{:S(2)}) collective-permute-start(bf16[192,1024]{1,0:T(8,128)(2,1)S(1)} %get-tuple-element.53), channel_id=1, source_target_pairs={{0,1},{1,0},{2,3},{3,2},{4,5},{5,4},{6,7},{7,6},{8,9},{9,8},{10,11... | collective-permute-start | bytes 1179656 | tf_op jit(solution)/shard_map/ppermute | solution.py:34
  356.6 15.5 %collective-permute-start.12 = (bf16[192,1024]{1,0:T(8,128)(2,1)S(1)}, bf16[192,1024]{1,0:T(8,128)(2,1)S(1)}, u32[]{:S(2)}, u32[]{:S(2)}) collective-permute-start(bf16[192,1024]{1,0:T(8,128)(2,1)S(1)} %get-tuple-element.58), channel_id=1, source_target_pairs={{0,2},{1,3},{2,0},{3,1},{4,6},{5,7},{6,4},{7,5},{8,10},{9,11},{10,... | collective-permute-start | bytes 1179656 | tf_op jit(solution)/shard_map/ppermute | solution.py:34
  357.2 21.1 %collective-permute-start.13 = (bf16[192,1024]{1,0:T(8,128)(2,1)S(1)}, bf16[192,1024]{1,0:T(8,128)(2,1)S(1)}, u32[]{:S(2)}, u32[]{:S(2)}) collective-permute-start(bf16[192,1024]{1,0:T(8,128)(2,1)S(1)} %get-tuple-element.57), channel_id=1, source_target_pairs={{0,3},{1,2},{2,1},{3,0},{4,7},{5,6},{6,5},{7,4},{8,11},{9,10},{10,... | collective-permute-start | bytes 1179656 | tf_op jit(solution)/shard_map/ppermute | solution.py:34
  361.7 20.8 %collective-permute-start.14 = (bf16[192,1024]{1,0:T(8,128)(2,1)S(1)}, bf16[192,1024]{1,0:T(8,128)(2,1)S(1)}, u32[]{:S(2)}, u32[]{:S(2)}) collective-permute-start(bf16[192,1024]{1,0:T(8,128)(2,1)S(1)} %get-tuple-element.56), channel_id=1, source_target_pairs={{0,1},{1,0},{2,3},{3,2},{4,5},{5,4},{6,7},{7,6},{8,9},{9,8},{10,11... | collective-permute-start | bytes 1179656 | tf_op jit(solution)/shard_map/ppermute | solution.py:34
  363.7 44.8 %collective-permute-start.21 = (f32[528,768]{1,0:T(8,128)S(1)}, f32[528,768]{1,0:T(8,128)S(1)}, u32[]{:S(2)}, u32[]{:S(2)}) collective-permute-start(f32[528,768]{1,0:T(8,128)S(1)} %slice.26.pc0_hbm), channel_id=1, source_target_pairs={{0,8},{1,9},{2,10},{3,11},{4,12},{5,13},{6,14},{7,15}} | collective-permute-start | bytes 4866056 | tf_op jit(solution)/shard_map/ppermute | solution.py:46
  372.1 23.6 %collective-permute-start.22 = (f32[240,768]{1,0:T(8,128)S(1)}, f32[240,768]{1,0:T(8,128)S(1)}, u32[]{:S(2)}, u32[]{:S(2)}) collective-permute-start(f32[240,768]{1,0:T(8,128)S(1)} %slice.27.pc1_hbm), channel_id=1, source_target_pairs={{12,8},{13,9},{14,10},{15,11},{4,0},{5,1},{6,2},{7,3}} | collective-permute-start | bytes 2211848 | tf_op jit(solution)/shard_map/ppermute | solution.py:51
  378.3 30.2 %collective-permute-start.19 = (f32[96,3072]{1,0:T(8,128)S(1)}, f32[96,3072]{1,0:T(8,128)S(1)}, u32[]{:S(2)}, u32[]{:S(2)}) collective-permute-start(f32[96,3072]{1,0:T(8,128)S(1)} %get-tuple-element.33.qb0_hbm), channel_id=1, source_target_pairs={{0,4},{1,5},{2,6},{3,7}} | collective-permute-start | bytes 3538952 | tf_op jit(solution)/shard_map/ppermute | solution.py:51
  382.5 26.0 %collective-permute-start.20 = (f32[96,3072]{1,0:T(8,128)S(1)}, f32[96,3072]{1,0:T(8,128)S(1)}, u32[]{:S(2)}, u32[]{:S(2)}) collective-permute-start(f32[96,3072]{1,0:T(8,128)S(1)} %get-tuple-element.34.qb1_hbm), channel_id=1, source_target_pairs={{12,4},{13,5},{14,6},{15,7}} | collective-permute-start | bytes 3538952 | tf_op jit(solution)/shard_map/ppermute | solution.py:46
  (28 other events, 514.1 us)
